TPU v7x, 32 devices: a whole 2x2x4 slice. The times are simulated.
32 devices in a mesh: rep: 2 (over x), seq: 16 (over z, y, core).
Axes of the slice: x: 2, y: 2, z: 4, core: 2. Of those that a mesh axis runs over, the one named last changes fastest.
Arguments:
- hidden: bfloat16 [128, 7168], P('rep'), parts along dimension 0
- w_query: bfloat16 [7168, 7168], replicated
- w_key: bfloat16 [7168, 1024], replicated
- w_value: bfloat16 [7168, 1024], replicated
- w_out: bfloat16 [7168, 7168], P('seq')
- k_cache: bfloat16 [128, 1024, 8, 128], P('rep', 'seq'), parts along dimension 0
- v_cache: bfloat16 [128, 1024, 8, 128], P('rep', 'seq'), parts along dimension 0
- positions: int32 [128], P('rep'), parts along dimension 0
Outputs:
- output 1: bfloat16 [128, 7168], P('rep'), parts along dimension 0
- output 2: bfloat16 [128, 1024, 8, 128], P('rep', 'seq'), parts along dimension 0
- output 3: bfloat16 [128, 1024, 8, 128], P('rep', 'seq'), parts along dimension 0
There are 2 independent parts. A program takes and returns all parts, laid end to end along the dimension named above; an argument that names none is the same for every part.
All inputs are finite; a program needn't handle non-finite values.
Results may differ from a plain program's by a relative error of at most 0.00603786.
Values are sent between devices in bfloat16 or wider.
A program may use at most 1 GiB of HBM per device.

v0:
```python
import jax
import jax.numpy as jnp
from jax import lax
from jax.sharding import PartitionSpec as P


def solution(mesh):
    cache_spec = P('rep', 'seq', None, None)
    in_specs = (P('rep', None), P(), P(), P(), P('seq', None), cache_spec, cache_spec, P('rep'))
    out_specs = (P('rep', None), cache_spec, cache_spec)

    def local_step(hidden, w_query, w_key, w_value, w_out, k_cache, v_cache, positions):
        batch_size, local_len, kv_heads, head_dim = k_cache.shape
        num_heads = w_query.shape[1] // head_dim
        group_size = num_heads // kv_heads
        shard_idx = lax.axis_index('seq')
        q_flat = jnp.dot(hidden, w_query, preferred_element_type=jnp.float32).astype(jnp.bfloat16)
        key_new = jnp.dot(hidden, w_key, preferred_element_type=jnp.float32).astype(jnp.bfloat16).reshape(batch_size, kv_heads, head_dim)
        value_new = jnp.dot(hidden, w_value, preferred_element_type=jnp.float32).astype(jnp.bfloat16).reshape(batch_size, kv_heads, head_dim)
        seq_ids = shard_idx * local_len + jnp.arange(local_len)
        at_pos = (seq_ids[None, :] == positions[:, None])[:, :, None, None]
        k_updated = jnp.where(at_pos, key_new[:, None], k_cache)
        v_updated = jnp.where(at_pos, value_new[:, None], v_cache)
        is_valid = (seq_ids[None, :] <= positions[:, None])[:, None, None, :]
        q_heads = q_flat.reshape(batch_size, kv_heads, group_size, head_dim)
        scores = jnp.einsum('bkgd,bskd->bkgs', q_heads, k_updated, preferred_element_type=jnp.float32) * head_dim ** -0.5
        scores = jnp.where(is_valid, scores, -jnp.inf)
        local_max = jnp.max(scores, axis=-1)
        safe_max = jnp.where(jnp.isfinite(local_max), local_max, 0.0)
        weights = jnp.exp(scores - safe_max[..., None])
        local_sum = jnp.sum(weights, axis=-1)
        local_out = jnp.einsum('bkgs,bskd->bkgd', weights.astype(jnp.bfloat16), v_updated, preferred_element_type=jnp.float32)
        global_max = lax.pmax(local_max, 'seq')
        rescale = jnp.exp(local_max - global_max)
        total_sum, total_out = lax.psum((local_sum * rescale, local_out * rescale[..., None]), 'seq')
        combined = (total_out / total_sum[..., None]).astype(jnp.bfloat16).reshape(batch_size, num_heads * head_dim)
        row_count = w_out.shape[0]
        combined_rows = lax.dynamic_slice_in_dim(combined, shard_idx * row_count, row_count, axis=1)
        part_out = jnp.dot(combined_rows, w_out, preferred_element_type=jnp.float32)
        result = lax.psum(part_out, 'seq').astype(jnp.bfloat16)
        return result, k_updated, v_updated

    return jax.shard_map(local_step, mesh=mesh, in_specs=in_specs, out_specs=out_specs, check_vma=False)
```

profile of v0, /device:TPU:0, one launch (start us, length us, event | category | flops | bytes accessed | tf_op | source)
XLA Modules:
  0.0 326.4 jit_solution(324622254772277513)
XLA Ops:
  7.2 0.0 copy-start
  7.2 0.0 all-reduce.3.cloned.1.call-start
  7.2 1.1 copy-done
  8.4 0.0 copy-start.3
  8.4 8.0 %fusion.10 = bf16[8,8,8,128]{3,1,2,0:T(8,128)(2,1)S(1)} fusion(bf16[64,7168]{1,0:T(8,128)(2,1)S(1)} %copy-done, bf16[7168,1024]{1,0:T(8,128)(2,1)} %param.10), kind=kOutput, calls=%fused_computation.16 | convolution fusion | flops 939589632 | bytes 15728640 | tf_op jit(solution)/shard_map/dot_general | solution.py:18
  16.4 1.3 copy-done.3
  17.7 2.7 fusion.11
  20.5 0.0 copy-start.5
  20.5 35.3 %convolution_convert_fusion = bf16[64,7168]{1,0:T(8,128)(2,1)S(1)} fusion(bf16[64,7168]{1,0:T(8,128)(2,1)S(1)} %copy-done, bf16[7168,7168]{1,0:T(8,128)(2,1)} %param.9), kind=kOutput, calls=%fused_computation.6 | convolution fusion | flops 6577127424 | bytes 104595456 | tf_op jit(solution)/shard_map/dot_general | solution.py:17
  55.8 2.2 reshape.73
  58.0 0.0 copy-done.5
  58.0 0.1 broadcast_compare_fusion.1
  58.1 0.0 copy-start.4
  58.1 9.6 %broadcast_select_fusion.1 = (bf16[64,64,8,128]{3,2,1,0:T(8,128)(2,1)S(1)}, bf16[64,64,8,128]{3,2,1,0:T(8,128)(2,1)}) fusion(bf16[64,64,8,128]{3,2,1,0:T(8,128)(2,1)} %param.13, pred[64,64]{1,0:T(8,128)(4,1)S(1)} %get-tuple-element.8, bf16[64,8,128]{2,1,0:T(8,128)(2,1)S(1)} %bitcast.14, bf16[64,64,8,128]{3,2,1,0:T(8,128)(2,1)} %param.14, ...), kind=kLoop, calls=%fused_computation.5 | loop fusion | flops 8388608 | bytes 33820672 | tf_op jit(solution)/shard_map/jit(_where)/select_n | solution.py:22
  67.7 0.0 copy-start.2
  67.7 0.0 copy-done.4
  67.7 4.5 %fusion.4 = (f32[64,8,7]{2,1,0:T(8,128)S(1)}, f32[64,8,7,64]{3,2,1,0:T(8,128)S(1)}) fusion(pred[64,64]{1,0:T(8,128)(4,1)S(1)} %get-tuple-element.7, bf16[64,8,7,128]{3,2,1,0:T(8,128)(2,1)S(1)} %copy-done.4, bf16[64,64,8,128]{3,2,1,0:T(8,128)(2,1)S(1)} %get-tuple-element.5), kind=kOutput, calls=%fused_computation.10 | convolution fusion | flops 59404800 | bytes 10242048 | tf_op jit(solution)/shard_map/bkgd,bskd->bkgs/dot_general | solution.py:26
  72.2 0.0 copy-done.2
  72.3 65.3 %pmax.7 = f32[64,8,7]{2,1,0:T(8,128)S(1)} all-reduce(f32[64,8,7]{2,1,0:T(8,128)S(1)} %get-tuple-element.9), channel_id=1, replica_groups=mesh['rep'=2,'seq'=16] {'seq'}, use_global_device_ids=true, to_apply=%region_1.2 | all-reduce | flops 3584 | bytes 28672 | tf_op jit(solution)/shard_map/pmax | solution.py:33
  137.6 1.3 fusion.5
  138.9 0.1 fusion.22
  139.0 5.8 %fusion.7 = f32[64,8,7,128]{3,2,1,0:T(8,128)} fusion(bf16[64,64,8,128]{3,2,1,0:T(8,128)(2,1)} %get-tuple-element.6, f32[64,8,7,64]{3,2,1,0:T(8,128)S(1)} %get-tuple-element.10, f32[64,8,7]{2,1,0:T(8,128)S(1)} %get-tuple-element.4, f32[64,8,7]{2,1,0:T(8,128)S(1)} %is-finite_select_fusion, pred[64,64]{1,0:T(8,128)(4,1)S(1)} %get-tuple-element.7), kind=kOutput, calls=%fused_computation.13 | convolution fusion | flops 60096512 | bytes 11173888 | tf_op jit(solution)/shard_map/bkgs,bskd->bkgd/dot_general | solution.py:32
  144.8 0.0 all-reduce.3.cloned.1.call-update
  144.8 61.2 %psum.22 = f32[64,8,7]{2,1,0:T(8,128)S(1)} all-reduce(f32[64,8,7]{2,1,0:T(8,128)S(1)} %get-tuple-element.3), channel_id=1, replica_groups=mesh['rep'=2,'seq'=16] {'seq'}, use_global_device_ids=true, to_apply=%region_4.5 | all-reduce | flops 3584 | bytes 28672 | tf_op jit(solution)/shard_map/psum | solution.py:35
  206.1 34.3 %all-reduce.3.cloned.1.call-done = f32[64,8,7,128]{3,2,1,0:T(8,128)} async-done(((f32[64,8,7,128]{3,2,1,0:T(8,128)}), f32[64,8,7,128]{3,2,1,0:T(8,128)}) %all-reduce.3.cloned.1.call-update) | async-done | bytes 1835024 | tf_op jit(solution)/shard_map/psum | solution.py:35
  240.4 1.9 divide_convert_fusion
  242.4 1.9 reshape.74
  244.3 0.0 copy-start.1
  244.3 4.2 %fusion.17 = f32[64,7168]{1,0:T(8,128)S(1)} fusion(bf16[448,7168]{1,0:T(8,128)(2,1)} %param.12, bf16[64,7168]{1,0:T(8,128)(2,1)} %reshape.74, s32[]{:T(128)S(6)} %select_n.26), kind=kOutput, calls=%fused_computation.24 | convolution fusion | flops 411041792 | bytes 8323076 | tf_op jit(solution)/shard_map/dot_general | solution.py:39
  248.5 71.1 %all-reduce.4 = bf16[64,7168]{1,0:T(8,128)(2,1)} all-reduce(f32[64,7168]{1,0:T(8,128)S(1)} %fusion.17), channel_id=1, replica_groups=mesh['rep'=2,'seq'=16] {'seq'}, use_global_device_ids=true, to_apply=%region_5.6 | all-reduce | flops 458752 | bytes 2752512 | tf_op jit(solution)/shard_map/psum | solution.py:40
  319.6 0.0 copy-done.1
  (4 shorter events, 0.1 us)
Async XLA Ops:
  7.2 1.2 copy-start
  7.2 233.2 %all-reduce.3.cloned.1.call-start = ((), (), s32[]{:S(2)}) async-start(), calls=%async_computation | async-start | bytes 4194304 | tf_op jit(solution)/shard_map/psum | solution.py:35
  8.4 9.3 %copy-start.3 = (bf16[7168,1024]{1,0:T(8,128)(2,1)S(1)}, bf16[7168,1024]{1,0:T(8,128)(2,1)}, u32[]{:S(2)}) copy-start(bf16[7168,1024]{1,0:T(8,128)(2,1)} %param.11) | copy-start | bytes 44040196
  20.5 37.6 %copy-start.5 = (s32[64]{0:T(128)S(1)}, s32[64]{0:T(128)}, u32[]{:S(2)}) copy-start(s32[64]{0:T(128)} %param.15) | copy-start | bytes 772
  58.1 9.6 %copy-start.4 = (bf16[64,8,7,128]{3,2,1,0:T(8,128)(2,1)S(1)}, bf16[64,8,7,128]{3,2,1,0:T(8,128)(2,1)}, u32[]{:S(2)}) copy-start(bf16[64,8,7,128]{3,2,1,0:T(8,128)(2,1)} %reshape.73) | copy-start | bytes 2752516
  67.7 4.5 %copy-start.2 = (bf16[64,64,8,128]{3,2,1,0:T(8,128)(2,1)}, bf16[64,64,8,128]{3,2,1,0:T(8,128)(2,1)S(1)}, u32[]{:S(2)}) copy-start(bf16[64,64,8,128]{3,2,1,0:T(8,128)(2,1)S(1)} %get-tuple-element.5) | copy-start | bytes 25165828
  244.3 75.3 %copy-start.1 = (bf16[64,7168]{1,0:T(8,128)(2,1)S(1)}, bf16[64,7168]{1,0:T(8,128)(2,1)}, u32[]{:S(2)}) copy-start(bf16[64,7168]{1,0:T(8,128)(2,1)} %param.8) | copy-start | bytes 2752516
Sparse Core Ops, SparseCore 0:
  144.9 95.4 all-reduce.2
where the time goes:
time: 327 us; the launch traced here: 326 us
  blocking collectives  198 us (61%)
  matrix products  60.6 us (19%)
  waiting for transfers between devices  34.4 us (11%)
  between operations  14.2 us (4%)
  other arithmetic  13 us (4%)
  local copies, waits for them, and re-layouts  6.63 us (2%)
    psum x1, blocking collectives, local_step(): result = lax.psum(part_out, 'seq').astype(jnp.bfloat16)  71.1 us
    pmax x1, blocking collectives, local_step(): global_max = lax.pmax(local_max, 'seq')  65.3 us
    psum x1, blocking collectives, local_step(): lax.psum((local_sum * rescale, local_out * rescale[..., None]), 'seq')  61.2 us
    dot_general x1, matrix products, local_step(): jnp.dot(hidden, w_query, preferred_element_type=jnp.float32)  35.3 us
    psum x1, waiting for transfers between devices, local_step(): lax.psum((local_sum * rescale, local_out * rescale[..., None]), 'seq')  34.3 us
    select_n x1, other arithmetic, local_step(): k_updated = jnp.where(at_pos, key_new[:, None], k_cache)  9.55 us
    dot_general x1, matrix products, local_step(): jnp.dot(hidden, w_key, preferred_element_type=jnp.float32)  7.98 us
  transfers between devices with their start and end apart: 1, of which 1 were waited for; matrix products, arithmetic and copies ran while one was open for 0% of the time, Pallas kernels for 0%

commit v1 on v0

v1 whole, which is shorter than its diff:
```python
import functools

import jax
import jax.numpy as jnp
from jax import lax
from jax.experimental import pallas as pl
from jax.experimental.pallas import tpu as pltpu
from jax.sharding import PartitionSpec as P

MESH = pl.DeviceIdType.MESH
F32, BF16 = jnp.float32, jnp.bfloat16
VMEM = pl.BlockSpec(memory_space=pltpu.VMEM)
ANY = pl.BlockSpec(memory_space=pl.ANY)
SMEM = pl.BlockSpec(memory_space=pltpu.SMEM)
LOWEST = float(jnp.finfo(jnp.float32).min)
D = 7168
HALF = D // 2
ROWS = 448
CHUNKS = 7
CHUNK = D // CHUNKS


class Place:
    def __init__(self):
        self.rep = lax.axis_index('rep')
        seq = lax.axis_index('seq')
        self.z = seq // 4
        self.y = lax.rem(seq // 2, 2)
        self.c = lax.rem(seq, 2)
        self.j = seq // 2

    def at(self, z, y, c):
        return (self.rep, (z * 2 + y) * 2 + c)

    def others(self):
        z = self.z
        return [lax.rem(z + 2, 4), 3 - z, z + 1 - 2 * lax.rem(z, 2), z]

    def greet(self):
        barrier = pltpu.get_barrier_semaphore()
        peers = [self.at(self.z, self.y, 1 - self.c), self.at(self.z, 1 - self.y, self.c)]
        peers += [self.at(zz, self.y, self.c) for zz in self.others()[:3]]
        for peer in peers:
            pl.semaphore_signal(barrier, inc=1, device_id=peer, device_id_type=MESH)
        pl.semaphore_wait(barrier, len(peers))


def push(src, dst, send, recv, device):
    copy = pltpu.make_async_remote_copy(
        src_ref=src, dst_ref=dst, send_sem=send, recv_sem=recv, device_id=device, device_id_type=MESH)
    return copy


def gather(me, region, other, sems):
    z_send, z_recv, y_send, y_recv, c_send, c_recv = sems
    zs = me.others()
    partner = me.at(me.z, me.y, 1 - me.c)
    y_peer = me.at(me.z, 1 - me.y, me.c)
    started = []

    def go(copy):
        copy.start()
        started.append(copy)
        return copy

    def to_partner(i, j):
        go(push(region(j), region(j), c_send.at[i], c_recv.at[i], partner))

    own = region(me.j)
    for i in range(3):
        go(push(own, own, z_send.at[i], z_recv.at[i], me.at(zs[i], me.y, me.c)))
    go(push(own, own, y_send.at[3], y_recv.at[3], y_peer))
    to_partner(3, me.j)
    for i in (2, 0, 1):
        src = region(zs[i] * 2 + me.y)
        push(src, src, z_send.at[i], z_recv.at[i], y_peer).wait_recv()
        go(push(src, src, y_send.at[i], y_recv.at[i], y_peer))
        to_partner(i, zs[i] * 2 + me.y)
    for i in (3, 2, 0, 1):
        j = zs[i] * 2 + 1 - me.y
        src = region(j)
        push(src, src, y_send.at[i], y_recv.at[i], y_peer).wait_recv()
        to_partner(4 + i, j)
    for i in (3, 2, 0, 1):
        for k, j in ((i, zs[i] * 2 + me.y), (4 + i, zs[i] * 2 + 1 - me.y)):
            dst = other(j)
            push(dst, dst, c_send.at[k], c_recv.at[k], partner).wait_recv()
    for copy in started:
        copy.wait_send()


GATHER_SEMS = [pltpu.SemaphoreType.DMA((3,)), pltpu.SemaphoreType.DMA((3,)), pltpu.SemaphoreType.DMA((4,)),
               pltpu.SemaphoreType.DMA((4,)), pltpu.SemaphoreType.DMA((8,)), pltpu.SemaphoreType.DMA((8,))]


def project_kernel(x, wq, wk, wv, wo, g, wox, wbuf, w_sem, wo_send, wo_recv, *sems):
    me = Place()

    def weights(c, i):
        rows = pl.ds(i * CHUNK, CHUNK)
        if c == 0:
            parts = [(wq.at[rows, pl.ds(pl.multiple_of(me.j * 896, 128), 640)], 0, 640)]
        else:
            parts = [(wq.at[rows, pl.ds(pl.multiple_of(me.j * 896 + 640, 128), 256)], 0, 256),
                     (wk.at[rows, pl.ds(pl.multiple_of(me.j * 128, 128), 128)], 256, 128),
                     (wv.at[rows, pl.ds(pl.multiple_of(me.j * 128, 128), 128)], 384, 128)]
        return [pltpu.make_async_copy(src, wbuf.at[rows, lo:lo + n], w_sem.at[i, k])
                for k, (src, lo, n) in enumerate(parts)]

    for c in range(2):
        @pl.when(me.c == c)
        def _(c=c):
            for i in range(CHUNKS):
                for copy in weights(c, i):
                    copy.start()

    me.greet()

    for c, lo, n in ((0, 0, 5), (1, 5, 4)):
        @pl.when(me.c == c)
        def _(c=c, lo=lo, n=n):
            acc = jnp.zeros((64, n * 128), F32)
            for i in range(CHUNKS):
                for copy in weights(c, i):
                    copy.wait()
                acc += jnp.dot(x[:, i * CHUNK:(i + 1) * CHUNK], wbuf[i * CHUNK:(i + 1) * CHUNK, :n * 128],
                               preferred_element_type=F32)
            for t in range(n):
                g[me.j, lo + t] = acc[:, t * 128:(t + 1) * 128].astype(BF16)

    swap = push(wo.at[:, pl.ds(pl.multiple_of((1 - me.c) * HALF, 128), HALF)], wox, wo_send, wo_recv,
                me.at(me.z, me.y, 1 - me.c))
    swap.start()
    for c in range(2):
        @pl.when(me.c == c)
        def _(c=c):
            parts = [lambda j: g.at[j, 0:5], lambda j: g.at[j, 5:9]]
            gather(me, parts[c], parts[1 - c], sems)
    swap.wait()


def attend_kernel(pos, g, k_in, v_in, k, v, ko, vo, o, stats, qs, vs, k_sem, v_sem):
    first = lax.axis_index('seq') * 64
    lane = lax.broadcasted_iota(jnp.int32, (8, 128), 1)
    is_head = [lax.rem(lane, 8) == h for h in range(8)]
    s_of = lane // 8

    def update(b):
        at = pos[b] - first
        mine = jnp.logical_and(at >= 0, at < 64)
        rows = pl.ds(pl.multiple_of(jnp.clip(at, 0, 63) * 8, 8), 8)
        new_k = qs[pl.ds(7 * 64 + b, 8, stride=512), :].astype(BF16)
        new_v = vs[pl.ds(b, 8, stride=64), :].astype(BF16)
        k[b, rows, :] = jnp.where(mine, new_k, k[b, rows, :])
        v[b, rows, :] = jnp.where(mine, new_v, v[b, rows, :])

    def out(i):
        bs = pl.ds(i * 16, 16)
        return [pltpu.make_async_copy(k.at[bs], ko.at[bs], k_sem.at[i]),
                pltpu.make_async_copy(v.at[bs], vo.at[bs], v_sem.at[i])]

    def spread(j, _):
        for t in range(8):
            qs[pl.ds(pl.multiple_of((j * 8 + t) * 64, 64), 64), :] = g[j, t].astype(F32)
        vs[pl.ds(pl.multiple_of(j * 64, 64), 64), :] = g[j, 8].astype(F32)
        return 0

    lax.fori_loop(0, 8, spread, 0)
    lax.fori_loop(0, 64, lambda b, _: (update(b), 0)[1], 0)

    def one(b):
        q = qs[pl.ds(b, 64, stride=64), :].astype(BF16)
        s = lax.dot_general(q, k[b], (((1,), (1,)), ((), ())), preferred_element_type=F32)
        limit = pos[b] - first
        valid, t = [], []
        for n in range(4):
            sn = s[:, n * 128:(n + 1) * 128]
            tn = sn[0:8]
            for h in range(1, 8):
                tn = jnp.where(is_head[h], sn[h * 8:h * 8 + 8], tn)
            ok = s_of + n * 16 <= limit
            valid.append(ok)
            t.append(jnp.where(ok, tn * (128 ** -0.5), LOWEST))
        m = jnp.maximum(jnp.maximum(t[0], t[1]), jnp.maximum(t[2], t[3]))
        for shift in (8, 16, 32, 64):
            m = jnp.maximum(m, pltpu.roll(m, shift, 1))
        p = [jnp.where(ok, jnp.exp(tn - m), 0.0) for ok, tn in zip(valid, t)]
        l = (p[0] + p[1]) + (p[2] + p[3])
        for shift in (8, 16, 32, 64):
            l = l + pltpu.roll(l, shift, 1)
        w = jnp.concatenate(
            [jnp.concatenate([jnp.where(is_head[h], pn, 0.0) for h in range(8)], axis=0) for pn in p],
            axis=1).astype(BF16)
        ob = jnp.dot(w, v[b], preferred_element_type=F32)
        for h in range(8):
            o[h, b] = ob[h * 8:h * 8 + 8]
        return m, l

    for i in range(4):
        for copy in out(i):
            copy.start()

    def group(i, _):
        def some(u, carry):
            ms, ls = carry
            for e in range(4):
                bb = u * 4 + e
                m, l = one(i * 16 + bb)
                here = s_of == bb
                ms, ls = jnp.where(here, m, ms), jnp.where(here, l, ls)
            return ms, ls
        zero = jnp.zeros((8, 128), F32)
        ms, ls = lax.fori_loop(0, 4, some, (zero, zero))
        stats[0, i] = ms
        stats[1, i] = ls
        return 0

    lax.fori_loop(0, 4, group, 0)
    for i in range(4):
        for copy in out(i):
            copy.wait()


def combine_kernel(o, stats, wo, wox, out, ra, sa, ma, sma, rb, sb, mb, smb, rc, sc, fin, lhs, wbuf, p, rb2, mb2, rc2,
                   w_sem, a_send, a_recv, b_send, b_recv, c_send, c_recv, d_send, d_recv, b2_send, b2_recv, c2_send,
                   c2_recv, *sems):
    me = Place()
    zs = me.others()
    partner = me.at(me.z, me.y, 1 - me.c)
    y_peer = me.at(me.z, 1 - me.y, me.c)
    z_peers = [me.at(zs[i], me.y, me.c) for i in range(3)]
    mine = pl.ds(pl.multiple_of(me.c * 32, 32), 32)
    theirs = pl.ds(pl.multiple_of((1 - me.c) * 32, 32), 32)
    started = []

    def go(copy):
        copy.start()
        started.append(copy)

    w_copies = [
        pltpu.make_async_copy(wo.at[:, pl.ds(pl.multiple_of(me.c * HALF, 128), HALF)],
                              wbuf.at[pl.ds(pl.multiple_of(me.c * ROWS, 64), ROWS)], w_sem.at[0]),
        pltpu.make_async_copy(wox, wbuf.at[pl.ds(pl.multiple_of((1 - me.c) * ROWS, 64), ROWS)], w_sem.at[1])]
    for copy in w_copies:
        copy.start()
    me.greet()

    order = [zs[i] * 2 + 1 - me.y for i in range(4)] + [zs[i] * 2 + me.y for i in range(4)]
    a_stat = push(stats.at[:, pl.ds((1 - me.c) * 2, 2)], sa, a_send.at[8], a_recv.at[8], partner)
    go(a_stat)
    a = [push(o.at[order[i], theirs], ra.at[i], a_send.at[i], a_recv.at[i], partner) for i in range(8)]
    for copy in a:
        go(copy)

    def weights_of(m_list, l_list):
        top = m_list[0]
        for m in m_list[1:]:
            top = jnp.maximum(top, m)
        scale = [jnp.exp(m - top) for m in m_list]
        total = scale[0] * l_list[0]
        for f, l in zip(scale[1:], l_list[1:]):
            total = total + f * l
        return top, total, scale

    def merge(h, scale, sources, store):
        for half in range(2):
            turned = [pltpu.roll(f[half], lax.rem(128 - h, 128), 1) for f in scale]
            for bb in range(16):
                b = half * 16 + bb
                total = None
                for f, source in zip(turned, sources):
                    term = source(b) * jnp.broadcast_to(f[:, bb * 8:bb * 8 + 1], (8, 128))
                    total = term if total is None else total + term
                store(b, total)

    a_stat.wait_recv()
    own = [[stats[s, me.c * 2 + half] for half in range(2)] for s in range(2)]
    scale_a = [[], []]
    for half in range(2):
        top, total, scale = weights_of([own[0][half], sa[0, half]], [own[1][half], sa[1, half]])
        sma[0, half], sma[1, half] = top, total
        scale_a[0].append(scale[0])
        scale_a[1].append(scale[1])
    b_stat = push(sma, sb, b_send.at[4], b_recv.at[4], y_peer)
    go(b_stat)

    def put(ref, i):
        def store(b, value):
            ref[i, b] = value
        return store

    b_copies = [push(ma.at[i], rb.at[i], b_send.at[i], b_recv.at[i], y_peer) for i in range(4)]
    for i in range(8):
        a[i].wait_recv()
        merge(order[i], scale_a,
              [lambda b, i=i: o[order[i], me.c * 32 + b], lambda b, i=i: ra[i, b]], put(ma, i))
        if i < 4:
            go(b_copies[i])

    b_stat.wait_recv()
    scale_b = [[], []]
    for half in range(2):
        top, total, scale = weights_of([sma[0, half], sb[0, half]], [sma[1, half], sb[1, half]])
        smb[0, half], smb[1, half] = top, total
        scale_b[0].append(scale[0])
        scale_b[1].append(scale[1])
    c_stats = [push(smb, sc.at[i], c_send.at[3 + i], c_recv.at[3 + i], z_peers[i]) for i in range(3)]
    for copy in c_stats:
        go(copy)
    c_copies = [push(mb.at[i], rc.at[i], c_send.at[i], c_recv.at[i], z_peers[i]) for i in range(3)]
    for i in range(4):
        b_copies[i].wait_recv()
        merge(order[4 + i], scale_b,
              [lambda b, i=i: ma[4 + i, b], lambda b, i=i: rb[i, b]], put(mb, i))
        if i < 3:
            go(c_copies[i])

    for i in range(3):
        c_stats[i].wait_recv()
    scale_c = [[], [], [], []]
    for half in range(2):
        _, total, scale = weights_of([smb[0, half]] + [sc[i, 0, half] for i in range(3)],
                                     [smb[1, half]] + [sc[i, 1, half] for i in range(3)])
        for s in range(4):
            scale_c[s].append(scale[s] / total)
    for i in range(3):
        c_copies[i].wait_recv()

    def final(b, value):
        fin[b * 8:b * 8 + 8, :] = value

    merge(order[7], scale_c, [lambda b: mb[3, b]] + [lambda b, i=i: rc[i, b] for i in range(3)], final)
    for t in range(7):
        lhs[mine, t * 128:(t + 1) * 128] = fin[pl.ds(t, 32, stride=8), :].astype(BF16)
    d_copy = push(lhs.at[mine], lhs.at[mine], d_send, d_recv, partner)
    go(d_copy)
    for copy in w_copies:
        copy.wait()
    push(lhs.at[theirs], lhs.at[theirs], d_send, d_recv, partner).wait_recv()

    def columns(n, _):
        cols = pl.ds(pl.multiple_of(n * 512, 512), 512)
        p[:, cols] = jnp.dot(lhs[...], wbuf[:, cols], preferred_element_type=F32)
        return 0

    lax.fori_loop(0, 7, columns, 0)

    def rows_of(j):
        return pl.ds(pl.multiple_of(j * 8, 8), 8)

    b2 = [push(p.at[rows_of(order[i])], rb2.at[i], b2_send.at[i], b2_recv.at[i], y_peer) for i in range(4)]
    c2 = [push(mb2.at[i], rc2.at[i], c2_send.at[i], c2_recv.at[i], z_peers[i]) for i in range(3)]
    for copy in b2:
        go(copy)
    for i in range(4):
        b2[i].wait_recv()
        mb2[i] = p[rows_of(order[4 + i]), :] + rb2[i]
        if i < 3:
            go(c2[i])
    for i in range(3):
        c2[i].wait_recv()
    total = (mb2[3] + rc2[2]) + (rc2[0] + rc2[1])
    out[rows_of(me.j), pl.ds(pl.multiple_of(me.c * HALF, 128), HALF)] = total.astype(BF16)

    def part(j, c):
        return out.at[rows_of(j), pl.ds(pl.multiple_of(c * HALF, 128), HALF)]

    gather(me, lambda j: part(j, me.c), lambda j: part(j, 1 - me.c), sems)
    for copy in started:
        copy.wait_send()


def dma(*shape):
    return pltpu.SemaphoreType.DMA(shape) if shape else pltpu.SemaphoreType.DMA


def solution(mesh):
    cache_spec = P('rep', 'seq', None, None)
    in_specs = (P('rep', None), P(), P(), P(), P('seq', None), cache_spec, cache_spec, P('rep'))
    out_specs = (P('rep', None), cache_spec, cache_spec)
    shape = jax.ShapeDtypeStruct

    def step(x, wq, wk, wv, wo, k, v, pos):
        g, wox = pl.pallas_call(
            project_kernel,
            out_shape=[shape((8, 9, 64, 128), BF16), shape((ROWS, HALF), BF16)],
            in_specs=[VMEM, ANY, ANY, ANY, ANY],
            out_specs=[VMEM, ANY],
            scratch_shapes=[pltpu.VMEM((D, 640), BF16), dma(CHUNKS, 3), dma(), dma()] + GATHER_SEMS,
            cost_estimate=pl.CostEstimate(flops=10 ** 10, bytes_accessed=10 ** 7, transcendentals=0),
            compiler_params=pltpu.CompilerParams(
                collective_id=1, has_side_effects=True, vmem_limit_bytes=16 * 2 ** 20),
            name='project',
        )(x, wq, wk, wv, wo)
        k2 = pltpu.with_memory_space_constraint(k.reshape(64, 512, 128), pltpu.VMEM)
        v2 = pltpu.with_memory_space_constraint(v.reshape(64, 512, 128), pltpu.VMEM)
        cache = (64, 512, 128)
        _, _, ko, vo, o, stats = pl.pallas_call(
            attend_kernel,
            out_shape=[pltpu.VMEM(cache, BF16), pltpu.VMEM(cache, BF16), shape(cache, BF16), shape(cache, BF16),
                       shape((8, 64, 8, 128), F32), shape((2, 4, 8, 128), F32)],
            in_specs=[SMEM, VMEM, VMEM, VMEM],
            out_specs=[VMEM, VMEM, ANY, ANY, VMEM, VMEM],
            input_output_aliases={2: 0, 3: 1},
            scratch_shapes=[pltpu.VMEM((4096, 128), F32), pltpu.VMEM((512, 128), F32), dma(4), dma(4)],
            cost_estimate=pl.CostEstimate(flops=2 * 10 ** 9, bytes_accessed=4 * 10 ** 7, transcendentals=0),
            compiler_params=pltpu.CompilerParams(vmem_limit_bytes=30 * 2 ** 20),
            name='attend',
        )(pos, g, k2, v2)
        piece = (32, 8, 128)
        stat = (2, 2, 8, 128)
        y = pl.pallas_call(
            combine_kernel,
            out_shape=shape((64, D), BF16),
            in_specs=[VMEM, VMEM, ANY, ANY],
            out_specs=VMEM,
            scratch_shapes=[
                pltpu.VMEM((8,) + piece, F32), pltpu.VMEM(stat, F32), pltpu.VMEM((8,) + piece, F32),
                pltpu.VMEM(stat, F32),
                pltpu.VMEM((4,) + piece, F32), pltpu.VMEM(stat, F32), pltpu.VMEM((4,) + piece, F32),
                pltpu.VMEM(stat, F32),
                pltpu.VMEM((3,) + piece, F32), pltpu.VMEM((3,) + stat, F32),
                pltpu.VMEM((256, 128), F32), pltpu.VMEM((64, 896), BF16), pltpu.VMEM((896, HALF), BF16),
                pltpu.VMEM((64, HALF), F32), pltpu.VMEM((4, 8, HALF), F32), pltpu.VMEM((4, 8, HALF), F32),
                pltpu.VMEM((3, 8, HALF), F32),
                dma(2), dma(9), dma(9), dma(5), dma(5), dma(6), dma(6), dma(), dma(), dma(4), dma(4), dma(3), dma(3),
            ] + GATHER_SEMS,
            cost_estimate=pl.CostEstimate(flops=10 ** 10, bytes_accessed=10 ** 7, transcendentals=0),
            compiler_params=pltpu.CompilerParams(
                collective_id=2, has_side_effects=True, vmem_limit_bytes=28 * 2 ** 20),
            name='combine',
        )(o, stats, wo, wox)
        return y, ko.reshape(k.shape), vo.reshape(v.shape)

    return jax.shard_map(step, mesh=mesh, in_specs=in_specs, out_specs=out_specs, check_vma=False)
```

time: 327 us -> 140 us (0.43)
  blocking collectives: 198 us -> 0 us
  Pallas kernels: 0 us -> 109 us
  matrix products: 60.6 us -> 0 us
  waiting for transfers between devices: 34.4 us -> 0 us
  local copies, waits for them, and re-layouts: 6.63 us -> 30.8 us
  between operations: 14.2 us -> 0.7 us
  other arithmetic: 13 us -> 0.01 us
    psum x2 -> x0, blocking collectives: 132 us -> none  [the longest x1 71.1 us: local_step(): result = lax.psum(part_out, 'seq').astype(jnp.bfloat16)]
    pallas_call x0 -> x3, Pallas kernels: none -> 109 us  [the longest x1 52.2 us: step(): pl.pallas_call(combine_kernel, out_shape=shape((64, D), BF16), in_specs=[...]
    pmax x1 -> x0, blocking collectives: 65.3 us -> none  [local_step(): global_max = lax.pmax(local_max, 'seq')]
    dot_general x6 -> x0, matrix products: 60.6 us -> none  [the longest x1 35.3 us: local_step(): jnp.dot(hidden, w_query, preferred_element_type=jnp.float32)]
    psum x1 -> x0, waiting for transfers between devices: 34.3 us -> none  [local_step(): lax.psum((local_sum * rescale, local_out * rescale[..., None]), 'seq')]
    unnamed x14 -> x19, local copies, waits for them, and re-layouts: 2.52 us -> 30.8 us
    select_n x2 -> x0, other arithmetic: 9.58 us -> none  [the longest x1 9.55 us: local_step(): k_updated = jnp.where(at_pos, key_new[:, None], k_cache)]
    reshape x2 -> x0, local copies, waits for them, and re-layouts: 4.11 us -> none  [the longest x1 2.21 us: local_step(): q_heads = q_flat.reshape(batch_size, kv_heads, group_size, head_dim)]
  transfers between devices with their start and end apart: 1 -> 0, of which waited for: 1 -> 0; matrix products, arithmetic and copies ran while one was open for 0% -> 0% of each run, Pallas kernels for 0% -> 0%
where the time goes in v1:
time: 140 us
  Pallas kernels  109 us (78%)
  local copies, waits for them, and re-layouts  30.8 us (22%)
    pallas_call x1, Pallas kernels, step(): pl.pallas_call(combine_kernel, out_shape=shape((64, D), BF16), in_specs=[...  52.2 us
    pallas_call x1, Pallas kernels, step(): pl.pallas_call(attend_kernel, out_shape=[pltpu.VMEM(cache, BF16), pltpu.V...  36.1 us
    unnamed x19, local copies, waits for them, and re-layouts  30.8 us
    pallas_call x1, Pallas kernels, step(): pl.pallas_call(project_kernel, out_shape=[shape((8, 9, 64, 128), BF16), s...  20.3 us

profile of v1, /device:TPU:0, one launch (start us, length us, event | category | flops | bytes accessed | tf_op | source)
XLA Modules:
  0.0 140.1 jit_solution(15493995833472419616)
XLA Ops:
  0.6 7.8 %copy.19 = bf16[64,64,8,128]{3,2,1,0:T(8,128)(2,1)} copy(bf16[64,64,8,128]{3,2,1,0:T(8,128)(2,1)} %param.14) | data formatting | bytes 16777216
  8.4 0.0 copy-start.4
  8.4 0.0 slice-start
  8.4 7.9 %copy.18 = bf16[64,64,8,128]{3,2,1,0:T(8,128)(2,1)} copy(bf16[64,64,8,128]{3,2,1,0:T(8,128)(2,1)} %param.13) | data formatting | bytes 16777216
  16.3 0.0 copy-done.4
  16.3 0.0 copy-start.1
  16.3 5.2 %copy-done.1 = bf16[7168,1024]{1,0:T(8,128)(2,1)S(1)} copy-done((bf16[7168,1024]{1,0:T(8,128)(2,1)S(1)}, bf16[7168,1024]{1,0:T(8,128)(2,1)}, u32[]{:S(2)}) %copy-start.1) | copy-done | bytes 14680088
  21.5 0.0 copy-start.2
  21.5 2.8 %copy-done.2 = bf16[448,7168]{1,0:T(8,128)(2,1)S(1)} copy-done((bf16[448,7168]{1,0:T(8,128)(2,1)S(1)}, bf16[448,7168]{1,0:T(8,128)(2,1)}, u32[]{:S(2)}) %copy-start.2) | copy-done | bytes 6422552
  24.3 0.0 slice-start.1
  24.3 0.0 copy-start.5
  24.3 20.3 %project.1 = (bf16[8,9,64,128]{3,2,1,0:T(8,128)(2,1)S(1)}, bf16[448,3584]{1,0:T(8,128)(2,1)S(1)}) custom-call(bf16[64,7168]{1,0:T(8,128)(2,1)S(1)} %copy-done.4, bf16[7168,7168]{1,0:T(8,128)(2,1)} %wq.1, bf16[7168,1024]{1,0:T(8,128)(2,1)S(1)} %copy-done.1, bf16[7168,1024]{1,0:T(8,128)(2,1)} %wv.1, bf16[448,7168]{1,0:T(8,128)(2,1)S(1)} %copy-done.2), custom_call_target="tpu_custom_call" | custom-call | flops 10000000000 | bytes 10000000 | tf_op jit(solution)/shard_map/project/pallas_call | solution.py:384
  44.6 0.0 slice-done
  44.6 0.0 slice-done.1
  44.7 0.0 copy-done.5
  44.7 0.0 copy-start
  44.7 3.4 %copy-done = bf16[64,64,8,128]{3,2,1,0:T(8,128)(2,1)S(1)} copy-done((bf16[64,64,8,128]{3,2,1,0:T(8,128)(2,1)S(1)}, bf16[64,64,8,128]{3,2,1,0:T(8,128)(2,1)}, u32[]{:S(2)}) %copy-start) | copy-done | bytes 8388632
  48.0 36.1 %attend.1 = (bf16[64,512,128]{2,1,0:T(8,128)(2,1)S(1)}, bf16[64,512,128]{2,1,0:T(8,128)(2,1)S(1)}, bf16[64,512,128]{2,1,0:T(8,128)(2,1)}, bf16[64,512,128]{2,1,0...) custom-call(s32[64]{0:T(128)S(1)} %copy-done.5, ...), custom_call_target="tpu_custom_call", output_to_operand_aliasing={{0}: (2, {}), {1}: (3, {})} | custom-call | flops 2000000000 | bytes 40000000 | tf_op jit(solution)/shard_map/attend/pallas_call | solution.py:398
  84.1 0.0 copy-start.3
  84.1 2.8 %copy-done.3 = bf16[448,7168]{1,0:T(8,128)(2,1)S(1)} copy-done((bf16[448,7168]{1,0:T(8,128)(2,1)S(1)}, bf16[448,7168]{1,0:T(8,128)(2,1)}, u32[]{:S(2)}) %copy-start.3) | copy-done | bytes 6422552
  86.9 52.2 %combine.1 = bf16[64,7168]{1,0:T(8,128)(2,1)S(1)} custom-call(f32[8,64,8,128]{3,2,1,0:T(8,128)S(1)} %get-tuple-element.10.o, f32[2,4,8,128]{3,2,1,0:T(8,128)S(1)} %get-tuple-element.11.stats, bf16[448,7168]{1,0:T(8,128)(2,1)S(1)} %copy-done.3, bf16[448,3584]{1,0:T(8,128)(2,1)S(1)} %get-tuple-element.12.wox), custom_call_target="tpu_custom_call" | custom-call | flops 10000000000 | bytes 10000000 | tf_op jit(solution)/shard_map/combine/pallas_call | solution.py:412
  139.2 0.9 copy.20
  (1 shorter events, 0.0 us)
Async XLA Ops:
  8.4 7.9 %copy-start.4 = (bf16[64,7168]{1,0:T(8,128)(2,1)S(1)}, bf16[64,7168]{1,0:T(8,128)(2,1)}, u32[]{:S(2)}) copy-start(bf16[64,7168]{1,0:T(8,128)(2,1)} %x.1) | copy-start | bytes 2752516
  8.4 36.2 %slice-start = ((s8[8388608]{0:T(1024)(128)(4,1)}), s8[4194304]{0:T(1024)(128)(4,1)S(1)}, s32[]{:S(2)}) async-start(s8[8388608]{0:T(1024)(128)(4,1)} %bitcast.4), calls=%async_computation | async-start | bytes 8388608
  16.3 5.2 %copy-start.1 = (bf16[7168,1024]{1,0:T(8,128)(2,1)S(1)}, bf16[7168,1024]{1,0:T(8,128)(2,1)}, u32[]{:S(2)}) copy-start(bf16[7168,1024]{1,0:T(8,128)(2,1)} %wk.1) | copy-start | bytes 44040196
  21.5 2.8 %copy-start.2 = (bf16[448,7168]{1,0:T(8,128)(2,1)S(1)}, bf16[448,7168]{1,0:T(8,128)(2,1)}, u32[]{:S(2)}) copy-start(bf16[448,7168]{1,0:T(8,128)(2,1)} %wo.3) | copy-start | bytes 19267588
  24.3 20.3 %slice-start.1 = ((s8[8388608]{0:T(1024)(128)(4,1)}), s8[4194304]{0:T(1024)(128)(4,1)S(1)}, s32[]{:S(2)}) async-start(s8[8388608]{0:T(1024)(128)(4,1)} %bitcast.4), calls=%async_computation.1 | async-start | bytes 8388608
  24.3 20.3 %copy-start.5 = (s32[64]{0:T(128)S(1)}, s32[64]{0:T(128)}, u32[]{:S(2)}) copy-start(s32[64]{0:T(128)} %pos.1) | copy-start | bytes 772
  44.7 3.4 %copy-start = (bf16[64,64,8,128]{3,2,1,0:T(8,128)(2,1)S(1)}, bf16[64,64,8,128]{3,2,1,0:T(8,128)(2,1)}, u32[]{:S(2)}) copy-start(bf16[64,64,8,128]{3,2,1,0:T(8,128)(2,1)} %copy.18) | copy-start | bytes 25165828
  84.1 2.8 %copy-start.3 = (bf16[448,7168]{1,0:T(8,128)(2,1)S(1)}, bf16[448,7168]{1,0:T(8,128)(2,1)}, u32[]{:S(2)}) copy-start(bf16[448,7168]{1,0:T(8,128)(2,1)} %wo.3) | copy-start | bytes 19267588

commit v2 on v1

--- a/solution.py
+++ b/solution.py
@@ -10,13 +10,15 @@
 MESH = pl.DeviceIdType.MESH
 F32, BF16 = jnp.float32, jnp.bfloat16
 VMEM = pl.BlockSpec(memory_space=pltpu.VMEM)
-ANY = pl.BlockSpec(memory_space=pl.ANY)
+HBM = pl.BlockSpec(memory_space=pltpu.HBM)
 SMEM = pl.BlockSpec(memory_space=pltpu.SMEM)
 LOWEST = float(jnp.finfo(jnp.float32).min)
 D = 7168
 HALF = D // 2
 ROWS = 448
 CHUNKS = 7
+BATCH = 8
+PITCH = 65
 CHUNK = D // CHUNKS
 
 
@@ -93,8 +95,9 @@
                pltpu.SemaphoreType.DMA((4,)), pltpu.SemaphoreType.DMA((8,)), pltpu.SemaphoreType.DMA((8,))]
 
 
-def project_kernel(x, wq, wk, wv, wo, g, wox, wbuf, w_sem, wo_send, wo_recv, *sems):
+def project_kernel(x, wq, wk, wv, wo, k_in, v_in, g, wox, k, v, wbuf, w_sem, kv_sem, wo_send, wo_recv, *sems):
     me = Place()
+    cache = [pltpu.make_async_copy(k_in, k, kv_sem.at[0]), pltpu.make_async_copy(v_in, v, kv_sem.at[1])]
 
     def weights(c, i):
         rows = pl.ds(i * CHUNK, CHUNK)
@@ -114,6 +117,8 @@
                 for copy in weights(c, i):
                     copy.start()
 
+    for copy in cache:
+        copy.start()
     me.greet()
 
     for c, lo, n in ((0, 0, 5), (1, 5, 4)):
@@ -137,6 +142,8 @@
             parts = [lambda j: g.at[j, 0:5], lambda j: g.at[j, 5:9]]
             gather(me, parts[c], parts[1 - c], sems)
     swap.wait()
+    for copy in cache:
+        copy.wait()
 
 
 def attend_kernel(pos, g, k_in, v_in, k, v, ko, vo, o, stats, qs, vs, k_sem, v_sem):
@@ -149,8 +156,8 @@
         at = pos[b] - first
         mine = jnp.logical_and(at >= 0, at < 64)
         rows = pl.ds(pl.multiple_of(jnp.clip(at, 0, 63) * 8, 8), 8)
-        new_k = qs[pl.ds(7 * 64 + b, 8, stride=512), :].astype(BF16)
-        new_v = vs[pl.ds(b, 8, stride=64), :].astype(BF16)
+        new_k = qs[pl.ds(7 * PITCH + b, 8, stride=8 * PITCH), :].astype(BF16)
+        new_v = vs[pl.ds(b, 8, stride=PITCH), :].astype(BF16)
         k[b, rows, :] = jnp.where(mine, new_k, k[b, rows, :])
         v[b, rows, :] = jnp.where(mine, new_v, v[b, rows, :])
 
@@ -161,15 +168,24 @@
 
     def spread(j, _):
         for t in range(8):
-            qs[pl.ds(pl.multiple_of((j * 8 + t) * 64, 64), 64), :] = g[j, t].astype(F32)
-        vs[pl.ds(pl.multiple_of(j * 64, 64), 64), :] = g[j, 8].astype(F32)
+            qs[pl.ds((j * 8 + t) * PITCH, 64), :] = g[j, t].astype(F32)
+        vs[pl.ds(j * PITCH, 64), :] = g[j, 8].astype(F32)
         return 0
 
-    lax.fori_loop(0, 8, spread, 0)
-    lax.fori_loop(0, 64, lambda b, _: (update(b), 0)[1], 0)
-
-    def one(b):
-        q = qs[pl.ds(b, 64, stride=64), :].astype(BF16)
+    lax.fori_loop(0, 8, spread, 0, unroll=2)
+
+    def updates(i, _):
+        for e in range(8):
+            update(i * 8 + e)
+        return 0
+
+    lax.fori_loop(0, 8, updates, 0)
+    for i in range(4):
+        for copy in out(i):
+            copy.start()
+
+    def scores(b):
+        q = qs[pl.ds(b, 64, stride=PITCH), :].astype(BF16)
         s = lax.dot_general(q, k[b], (((1,), (1,)), ((), ())), preferred_element_type=F32)
         limit = pos[b] - first
         valid, t = [], []
@@ -181,41 +197,44 @@
             ok = s_of + n * 16 <= limit
             valid.append(ok)
             t.append(jnp.where(ok, tn * (128 ** -0.5), LOWEST))
-        m = jnp.maximum(jnp.maximum(t[0], t[1]), jnp.maximum(t[2], t[3]))
+        return t, valid
+
+    def soften(batch):
+        m = [jnp.maximum(jnp.maximum(t[0], t[1]), jnp.maximum(t[2], t[3])) for t, _ in batch]
         for shift in (8, 16, 32, 64):
-            m = jnp.maximum(m, pltpu.roll(m, shift, 1))
-        p = [jnp.where(ok, jnp.exp(tn - m), 0.0) for ok, tn in zip(valid, t)]
-        l = (p[0] + p[1]) + (p[2] + p[3])
+            turned = [pltpu.roll(x, shift, 1) for x in m]
+            m = [jnp.maximum(x, y) for x, y in zip(m, turned)]
+        p = [[jnp.where(ok, jnp.exp(tn - x), 0.0) for tn, ok in zip(t, valid)] for (t, valid), x in zip(batch, m)]
+        l = [(q[0] + q[1]) + (q[2] + q[3]) for q in p]
         for shift in (8, 16, 32, 64):
-            l = l + pltpu.roll(l, shift, 1)
+            turned = [pltpu.roll(x, shift, 1) for x in l]
+            l = [x + y for x, y in zip(l, turned)]
+        return m, l, p
+
+    def values(b, p):
         w = jnp.concatenate(
             [jnp.concatenate([jnp.where(is_head[h], pn, 0.0) for h in range(8)], axis=0) for pn in p],
             axis=1).astype(BF16)
         ob = jnp.dot(w, v[b], preferred_element_type=F32)
         for h in range(8):
             o[h, b] = ob[h * 8:h * 8 + 8]
-        return m, l
-
-    for i in range(4):
-        for copy in out(i):
-            copy.start()
-
-    def group(i, _):
-        def some(u, carry):
-            ms, ls = carry
-            for e in range(4):
-                bb = u * 4 + e
-                m, l = one(i * 16 + bb)
-                here = s_of == bb
-                ms, ls = jnp.where(here, m, ms), jnp.where(here, l, ls)
-            return ms, ls
-        zero = jnp.zeros((8, 128), F32)
-        ms, ls = lax.fori_loop(0, 4, some, (zero, zero))
-        stats[0, i] = ms
-        stats[1, i] = ls
-        return 0
-
-    lax.fori_loop(0, 4, group, 0)
+
+    ahead = [scores(b) for b in range(BATCH)]
+    ms = ls = None
+    for i in range(64 // BATCH):
+        batch, ahead = ahead, []
+        if i + 1 < 64 // BATCH:
+            ahead = [scores((i + 1) * BATCH + e) for e in range(BATCH)]
+        m, l, p = soften(batch)
+        for e in range(BATCH):
+            b = i * BATCH + e
+            values(b, p[e])
+            bb = b % 16
+            ms = m[e] if bb == 0 else jnp.where(s_of == bb, m[e], ms)
+            ls = l[e] if bb == 0 else jnp.where(s_of == bb, l[e], ls)
+            if bb == 15:
+                stats[0, b // 16] = ms
+                stats[1, b // 16] = ls
     for i in range(4):
         for copy in out(i):
             copy.wait()
@@ -381,28 +400,27 @@
     shape = jax.ShapeDtypeStruct
 
     def step(x, wq, wk, wv, wo, k, v, pos):
-        g, wox = pl.pallas_call(
+        cache = (64, 512, 128)
+        g, wox, k2, v2 = pl.pallas_call(
             project_kernel,
-            out_shape=[shape((8, 9, 64, 128), BF16), shape((ROWS, HALF), BF16)],
-            in_specs=[VMEM, ANY, ANY, ANY, ANY],
-            out_specs=[VMEM, ANY],
-            scratch_shapes=[pltpu.VMEM((D, 640), BF16), dma(CHUNKS, 3), dma(), dma()] + GATHER_SEMS,
+            out_shape=[pltpu.VMEM((8, 9, 64, 128), BF16), shape((ROWS, HALF), BF16), pltpu.VMEM(cache, BF16),
+                       pltpu.VMEM(cache, BF16)],
+            in_specs=[VMEM, HBM, HBM, HBM, HBM, HBM, HBM],
+            out_specs=[VMEM, HBM, VMEM, VMEM],
+            scratch_shapes=[pltpu.VMEM((D, 640), BF16), dma(CHUNKS, 3), dma(2), dma(), dma()] + GATHER_SEMS,
             cost_estimate=pl.CostEstimate(flops=10 ** 10, bytes_accessed=10 ** 7, transcendentals=0),
             compiler_params=pltpu.CompilerParams(
-                collective_id=1, has_side_effects=True, vmem_limit_bytes=16 * 2 ** 20),
+                collective_id=1, has_side_effects=True, vmem_limit_bytes=32 * 2 ** 20),
             name='project',
-        )(x, wq, wk, wv, wo)
-        k2 = pltpu.with_memory_space_constraint(k.reshape(64, 512, 128), pltpu.VMEM)
-        v2 = pltpu.with_memory_space_constraint(v.reshape(64, 512, 128), pltpu.VMEM)
-        cache = (64, 512, 128)
+        )(x, wq, wk, wv, wo, k.reshape(cache), v.reshape(cache))
         _, _, ko, vo, o, stats = pl.pallas_call(
             attend_kernel,
             out_shape=[pltpu.VMEM(cache, BF16), pltpu.VMEM(cache, BF16), shape(cache, BF16), shape(cache, BF16),
                        shape((8, 64, 8, 128), F32), shape((2, 4, 8, 128), F32)],
             in_specs=[SMEM, VMEM, VMEM, VMEM],
-            out_specs=[VMEM, VMEM, ANY, ANY, VMEM, VMEM],
+            out_specs=[VMEM, VMEM, HBM, HBM, VMEM, VMEM],
             input_output_aliases={2: 0, 3: 1},
-            scratch_shapes=[pltpu.VMEM((4096, 128), F32), pltpu.VMEM((512, 128), F32), dma(4), dma(4)],
+            scratch_shapes=[pltpu.VMEM((64 * PITCH, 128), F32), pltpu.VMEM((8 * PITCH, 128), F32), dma(4), dma(4)],
             cost_estimate=pl.CostEstimate(flops=2 * 10 ** 9, bytes_accessed=4 * 10 ** 7, transcendentals=0),
             compiler_params=pltpu.CompilerParams(vmem_limit_bytes=30 * 2 ** 20),
             name='attend',
@@ -412,7 +430,7 @@
         y = pl.pallas_call(
             combine_kernel,
             out_shape=shape((64, D), BF16),
-            in_specs=[VMEM, VMEM, ANY, ANY],
+            in_specs=[VMEM, VMEM, HBM, HBM],
             out_specs=VMEM,
             scratch_shapes=[
                 pltpu.VMEM((8,) + piece, F32), pltpu.VMEM(stat, F32), pltpu.VMEM((8,) + piece, F32),
@@ -429,7 +447,7 @@
             compiler_params=pltpu.CompilerParams(
                 collective_id=2, has_side_effects=True, vmem_limit_bytes=28 * 2 ** 20),
             name='combine',
-        )(o, stats, wo, wox)
+        )(o, stats, pltpu.with_memory_space_constraint(wo, pltpu.HBM), wox)
         return y, ko.reshape(k.shape), vo.reshape(v.shape)
 
     return jax.shard_map(step, mesh=mesh, in_specs=in_specs, out_specs=out_specs, check_vma=False)

time: 140 us -> 89.3 us (0.64)
  local copies, waits for them, and re-layouts: 30.8 us -> 2.1 us
  Pallas kernels: 109 us -> 86.4 us
    unnamed x19 -> x5, local copies, waits for them, and re-layouts: 30.8 us -> 2.1 us
    pallas_call x1, Pallas kernels: 36.1 us -> 10.4 us  [step(): pl.pallas_call(attend_kernel, out_shape=[pltpu.VMEM(cache, BF16), pltpu.V...]
    pallas_call x1, Pallas kernels: 52.2 us -> 55.5 us  [step(): pl.pallas_call(combine_kernel, out_shape=shape((64, D), BF16), in_specs=[...]
where the time goes in v2:
time: 89.3 us; the launch traced here: 89.1 us
  Pallas kernels  86.4 us (97%)
  local copies, waits for them, and re-layouts  2.1 us (2%)
    pallas_call x1, Pallas kernels, step(): pl.pallas_call(combine_kernel, out_shape=shape((64, D), BF16), in_specs=[...  55.5 us
    pallas_call x1, Pallas kernels, step(): pl.pallas_call(project_kernel, out_shape=[pltpu.VMEM((8, 9, 64, 128), BF1...  20.5 us
    pallas_call x1, Pallas kernels, step(): pl.pallas_call(attend_kernel, out_shape=[pltpu.VMEM(cache, BF16), pltpu.V...  10.4 us
    unnamed x5, local copies, waits for them, and re-layouts  2.1 us

profile of v2, /device:TPU:0, one launch (start us, length us, event | category | flops | bytes accessed | tf_op | source)
XLA Modules:
  0.0 89.1 jit_solution(201024321635535437)
XLA Ops:
  0.6 0.0 copy-start
  0.6 1.2 %copy-done = bf16[64,7168]{1,0:T(8,128)(2,1)S(1)} copy-done((bf16[64,7168]{1,0:T(8,128)(2,1)S(1)}, bf16[64,7168]{1,0:T(8,128)(2,1)}, u32[]{:S(2)}) %copy-start) | copy-done | bytes 917528
  1.8 0.0 copy-start.1
  1.8 20.5 %project.1 = (bf16[8,9,64,128]{3,2,1,0:T(8,128)(2,1)S(1)}, bf16[448,3584]{1,0:T(8,128)(2,1)S(1)}, bf16[64,512,128]{2,1,0:T(8,128)(2,1)S(1)}, bf16[64,512,128]{2,1,0:T(8,128)(2,1)S(1)}) custom-call(bf16[64,7168]{1,0:T(8,128)(2,1)S(1)} %copy-done, bf16[7168,7168]{1,0:T(8,128)(2,1)} %wq.1, bf16[7168,1024]{1,0:T(8,128)(2,1)} %wk.1, bf16[7168,1024]{1,0:T(8,128)(2,1)} %wv.1, ...), custom_call_target="tpu_custom_call" | custom-call | flops 10000000000 | bytes 10000000 | tf_op jit(solution)/shard_map/project/pallas_call | solution.py:404
  22.3 0.0 copy-done.1
  22.3 10.4 %attend.1 = (bf16[64,512,128]{2,1,0:T(8,128)(2,1)S(1)}, bf16[64,512,128]{2,1,0:T(8,128)(2,1)S(1)}, bf16[64,512,128]{2,1,0:T(8,128)(2,1)}, bf16[64,512,128]{2,1,0...) custom-call(s32[64]{0:T(128)S(1)} %copy-done.1, ...), custom_call_target="tpu_custom_call", output_to_operand_aliasing={{0}: (2, {}), {1}: (3, {})} | custom-call | flops 2000000000 | bytes 40000000 | tf_op jit(solution)/shard_map/attend/pallas_call | solution.py:416
  32.7 55.5 %combine.1 = bf16[64,7168]{1,0:T(8,128)(2,1)S(1)} custom-call(f32[8,64,8,128]{3,2,1,0:T(8,128)S(1)} %get-tuple-element.14.o, f32[2,4,8,128]{3,2,1,0:T(8,128)S(1)} %get-tuple-element.15.stats, bf16[448,7168]{1,0:T(8,128)(2,1)} %wo.3, bf16[448,3584]{1,0:T(8,128)(2,1)S(1)} %get-tuple-element.16.wox), custom_call_target="tpu_custom_call" | custom-call | flops 10000000000 | bytes 10000000 | tf_op jit(solution)/shard_map/combine/pallas_call | solution.py:430
  88.2 0.9 %copy.16 = bf16[64,7168]{1,0:T(8,128)(2,1)} copy(bf16[64,7168]{1,0:T(8,128)(2,1)S(1)} %combine.1) | data formatting | bytes 1835008
Async XLA Ops:
  0.6 1.2 %copy-start = (bf16[64,7168]{1,0:T(8,128)(2,1)S(1)}, bf16[64,7168]{1,0:T(8,128)(2,1)}, u32[]{:S(2)}) copy-start(bf16[64,7168]{1,0:T(8,128)(2,1)} %x.1) | copy-start | bytes 2752516
  1.8 20.5 %copy-start.1 = (s32[64]{0:T(128)S(1)}, s32[64]{0:T(128)}, u32[]{:S(2)}) copy-start(s32[64]{0:T(128)} %pos.1) | copy-start | bytes 772

commit v3 on v2

v3 whole, which is shorter than its diff:
```python
import functools

import jax
import jax.numpy as jnp
from jax import lax
from jax.experimental import pallas as pl
from jax.experimental.pallas import tpu as pltpu
from jax.sharding import PartitionSpec as P

MESH = pl.DeviceIdType.MESH
F32, BF16 = jnp.float32, jnp.bfloat16
VMEM = pl.BlockSpec(memory_space=pltpu.VMEM)
HBM = pl.BlockSpec(memory_space=pltpu.HBM)
SMEM = pl.BlockSpec(memory_space=pltpu.SMEM)
LOWEST = float(jnp.finfo(jnp.float32).min)
D = 7168
HALF = D // 2
ROWS = 448
CHUNKS = 7
USED = slice(0, 7)
BATCH = 8
PITCH = 65
CHUNK = D // CHUNKS


class Place:
    def __init__(self):
        self.rep = lax.axis_index('rep')
        seq = lax.axis_index('seq')
        self.z = seq // 4
        self.y = lax.rem(seq // 2, 2)
        self.c = lax.rem(seq, 2)
        self.j = seq // 2

    def at(self, z, y, c):
        return (self.rep, (z * 2 + y) * 2 + c)

    def others(self):
        z = self.z
        low = 1 - z // 2
        return [low * 3, 1 + low, z + 1 - 2 * lax.rem(z, 2), z]

    def inner(self):
        return jnp.logical_and(self.z >= 1, self.z <= 2)

    def greet(self):
        barrier = pltpu.get_barrier_semaphore()
        peers = [self.at(self.z, self.y, 1 - self.c), self.at(self.z, 1 - self.y, self.c)]
        peers += [self.at(zz, self.y, self.c) for zz in self.others()[:3]]
        for peer in peers:
            pl.semaphore_signal(barrier, inc=1, device_id=peer, device_id_type=MESH)
        pl.semaphore_wait(barrier, len(peers))


def push(src, dst, send, recv, device):
    copy = pltpu.make_async_remote_copy(
        src_ref=src, dst_ref=dst, send_sem=send, recv_sem=recv, device_id=device, device_id_type=MESH)
    return copy


class Gather:
    def __init__(self, me, region, other, sems):
        self.me, self.region, self.other = me, region, other
        self.z_send, self.z_recv, self.y_send, self.y_recv, self.c_send, self.c_recv = sems
        self.zs = me.others()
        self.started = []

    def go(self, copy):
        copy.start()
        self.started.append(copy)

    def along_z(self, h, i, j, arrival=False):
        src = self.region(j, h)
        slot = i if arrival or i == 2 else lax.rem((self.me.z + 1) // 2, 2)
        return push(src, src, self.z_send.at[h, i], self.z_recv.at[h, slot],
                    self.me.at(self.zs[i], self.me.y, self.me.c))

    def across_y(self, h, i, j):
        src = self.region(j, h)
        return push(src, src, self.y_send.at[h, i], self.y_recv.at[h, i],
                    self.me.at(self.me.z, 1 - self.me.y, self.me.c))

    def to_core(self, h, i, src):
        return push(src, src, self.c_send.at[h, i], self.c_recv.at[h, i],
                    self.me.at(self.me.z, self.me.y, 1 - self.me.c))

    def start(self, h):
        for i in range(3):
            self.go(self.along_z(h, i, self.me.j))
        self.go(self.across_y(h, 3, self.me.j))
        self.go(self.to_core(h, 3, self.region(self.me.j, h)))

    def finish(self):
        near = [zz * 2 + self.me.y for zz in self.zs]
        far = [zz * 2 + 1 - self.me.y for zz in self.zs]
        for h in range(2):
            for i in (2, 1, 0):
                self.along_z(h, i, near[i], arrival=True).wait_recv()
                self.go(self.across_y(h, i, near[i]))
                self.go(self.to_core(h, i, self.region(near[i], h)))
        for h in range(2):
            for i in (3, 2, 1, 0):
                self.across_y(h, i, far[i]).wait_recv()
                self.go(self.to_core(h, 4 + i, self.region(far[i], h)))
        for h in range(2):
            for i in (3, 2, 1, 0):
                self.to_core(h, i, self.other(near[i], h)).wait_recv()
                self.to_core(h, 4 + i, self.other(far[i], h)).wait_recv()
        for copy in self.started:
            copy.wait_send()


GATHER_SEMS = [pltpu.SemaphoreType.DMA((2, n)) for n in (3, 3, 4, 4, 8, 8)]
TILES = (((0, 2), (2, 3)), ((5, 2), (7, 2)))


def project_kernel(x_in, wq, wk, wv, wo, k_in, v_in, g, wox, k, v, x, wbuf, x_sem, w_sem, kv_sem, wo_send, wo_recv,
                   *sems):
    me = Place()
    x_copy = pltpu.make_async_copy(x_in, x, x_sem)
    cache = [pltpu.make_async_copy(k_in, k, kv_sem.at[0]), pltpu.make_async_copy(v_in, v, kv_sem.at[1])]

    def weights(c, h, i):
        rows = pl.ds(i * CHUNK, CHUNK)
        lo, n = TILES[c][h]
        if lo < 7:
            parts = [(wq, me.j * 896 + lo * 128, n * 128)]
        else:
            parts = [(wk, me.j * 128, 128), (wv, me.j * 128, 128)]
        at = 256 * h
        copies = []
        for p, (w, col, width) in enumerate(parts):
            copies.append(pltpu.make_async_copy(w.at[rows, pl.ds(pl.multiple_of(col, 128), width)],
                                                wbuf.at[rows, at:at + width], w_sem.at[h, i, p]))
            at += width
        return copies

    for c in range(2):
        @pl.when(me.c == c)
        def _(c=c):
            for i in range(CHUNKS):
                for copy in weights(c, 0, i):
                    copy.start()
                if i == 0:
                    x_copy.start()
            for i in range(CHUNKS):
                for copy in weights(c, 1, i):
                    copy.start()

    for copy in cache:
        copy.start()
    me.greet()
    x_copy.wait()

    for c in range(2):
        @pl.when(me.c == c)
        def _(c=c):
            def region(c):
                return lambda j, h: g.at[j, TILES[c][h][0]:TILES[c][h][0] + TILES[c][h][1]]

            whole = Gather(me, region(c), region(1 - c), sems)
            for h in range(2):
                lo, n = TILES[c][h]
                acc = jnp.zeros((64, n * 128), F32)
                for i in range(CHUNKS):
                    for copy in weights(c, h, i):
                        copy.wait()
                    acc += jnp.dot(x[:, i * CHUNK:(i + 1) * CHUNK],
                                   wbuf[i * CHUNK:(i + 1) * CHUNK, 256 * h:256 * h + n * 128],
                                   preferred_element_type=F32)
                for t in range(n):
                    g[me.j, lo + t] = acc[:, t * 128:(t + 1) * 128].astype(BF16)
                whole.start(h)
            swap = push(wo.at[:, pl.ds(pl.multiple_of((1 - me.c) * HALF, 128), HALF)], wox, wo_send, wo_recv,
                        me.at(me.z, me.y, 1 - me.c))
            swap.start()
            whole.finish()
            swap.wait()
    for copy in cache:
        copy.wait()


def attend_kernel(pos, g, k_in, v_in, k, v, ko, vo, o, stats, qs, vs, k_sem, v_sem):
    first = lax.axis_index('seq') * 64
    lane = lax.broadcasted_iota(jnp.int32, (8, 128), 1)
    is_head = [lax.rem(lane, 8) == h for h in range(8)]
    s_of = lane // 8

    def update(b):
        at = pos[b] - first
        mine = jnp.logical_and(at >= 0, at < 64)
        rows = pl.ds(pl.multiple_of(jnp.clip(at, 0, 63) * 8, 8), 8)
        new_k = qs[pl.ds(7 * PITCH + b, 8, stride=8 * PITCH), :].astype(BF16)
        new_v = vs[pl.ds(b, 8, stride=PITCH), :].astype(BF16)
        k[b, rows, :] = jnp.where(mine, new_k, k[b, rows, :])
        v[b, rows, :] = jnp.where(mine, new_v, v[b, rows, :])

    def out(i):
        bs = pl.ds(i * 16, 16)
        return [pltpu.make_async_copy(k.at[bs], ko.at[bs], k_sem.at[i]),
                pltpu.make_async_copy(v.at[bs], vo.at[bs], v_sem.at[i])]

    def spread(j, _):
        for t in range(8):
            qs[pl.ds((j * 8 + t) * PITCH, 64), :] = g[j, t].astype(F32)
        vs[pl.ds(j * PITCH, 64), :] = g[j, 8].astype(F32)
        return 0

    lax.fori_loop(0, 8, spread, 0, unroll=2)

    def updates(i, _):
        for e in range(8):
            update(i * 8 + e)
        return 0

    lax.fori_loop(0, 8, updates, 0)
    for i in range(4):
        for copy in out(i):
            copy.start()

    def scores(b):
        q = qs[pl.ds(b, 64, stride=PITCH), :].astype(BF16)
        s = lax.dot_general(q, k[b], (((1,), (1,)), ((), ())), preferred_element_type=F32)
        limit = pos[b] - first
        valid, t = [], []
        for n in range(4):
            sn = s[:, n * 128:(n + 1) * 128]
            tn = sn[0:8]
            for h in range(1, 8):
                tn = jnp.where(is_head[h], sn[h * 8:h * 8 + 8], tn)
            ok = s_of + n * 16 <= limit
            valid.append(ok)
            t.append(jnp.where(ok, tn * (128 ** -0.5), LOWEST))
        return t, valid

    def soften(batch):
        m = [jnp.maximum(jnp.maximum(t[0], t[1]), jnp.maximum(t[2], t[3])) for t, _ in batch]
        for shift in (8, 16, 32, 64):
            turned = [pltpu.roll(x, shift, 1) for x in m]
            m = [jnp.maximum(x, y) for x, y in zip(m, turned)]
        p = [[jnp.where(ok, jnp.exp(tn - x), 0.0) for tn, ok in zip(t, valid)] for (t, valid), x in zip(batch, m)]
        l = [(q[0] + q[1]) + (q[2] + q[3]) for q in p]
        for shift in (8, 16, 32, 64):
            turned = [pltpu.roll(x, shift, 1) for x in l]
            l = [x + y for x, y in zip(l, turned)]
        return m, l, p

    def values(b, p):
        w = jnp.concatenate(
            [jnp.concatenate([jnp.where(is_head[h], pn, 0.0) for h in range(8)], axis=0) for pn in p],
            axis=1).astype(BF16)
        ob = jnp.dot(w, v[b], preferred_element_type=F32)
        for h in range(8):
            o[h, b] = ob[h * 8:h * 8 + 8]

    ahead = [scores(b) for b in range(BATCH)]
    ms = ls = None
    for i in range(64 // BATCH):
        batch, ahead = ahead, []
        if i + 1 < 64 // BATCH:
            ahead = [scores((i + 1) * BATCH + e) for e in range(BATCH)]
        m, l, p = soften(batch)
        for e in range(BATCH):
            b = i * BATCH + e
            values(b, p[e])
            bb = b % 16
            ms = m[e] if bb == 0 else jnp.where(s_of == bb, m[e], ms)
            ls = l[e] if bb == 0 else jnp.where(s_of == bb, l[e], ls)
            if bb == 15:
                stats[0, b // 16] = ms
                stats[1, b // 16] = ls
    for i in range(4):
        for copy in out(i):
            copy.wait()


def combine_kernel(o, stats, wo, wox, out, ra, sa, ma, sma, rb, sb, mb, smb, rm, sm, mc, smc, rf, sf, fin, lhs, wbuf, p,
                   rb2, mb2, rm2, mc2, rf2, w_sem, a_send, a_recv, b_send, b_recv, m_send, m_recv, f_send, f_recv,
                   s_send, s_recv, d_send, d_recv, b2_send, b2_recv, m2_send, m2_recv, f2_send, f2_recv, *sems):
    me = Place()
    zs = me.others()
    partner = me.at(me.z, me.y, 1 - me.c)
    y_peer = me.at(me.z, 1 - me.y, me.c)
    far_end, far_inner, mate = [me.at(zs[i], me.y, me.c) for i in range(3)]
    mine = pl.ds(pl.multiple_of(me.c * 32, 32), 32)
    theirs = pl.ds(pl.multiple_of((1 - me.c) * 32, 32), 32)
    started, at_end, at_inner = [], [], []

    def go(copy, kept=started):
        copy.start()
        kept.append(copy)

    def if_inner(f):
        pl.when(me.inner())(f)

    def if_end(f):
        pl.when(jnp.logical_not(me.inner()))(f)

    w_copies = [
        pltpu.make_async_copy(wo.at[:, pl.ds(pl.multiple_of(me.c * HALF, 128), HALF)],
                              wbuf.at[pl.ds(pl.multiple_of(me.c * ROWS, 64), ROWS)], w_sem.at[0]),
        pltpu.make_async_copy(wox, wbuf.at[pl.ds(pl.multiple_of((1 - me.c) * ROWS, 64), ROWS)], w_sem.at[1])]
    for copy in w_copies:
        copy.start()
    me.greet()

    order = [zs[i] * 2 + 1 - me.y for i in range(4)] + [zs[i] * 2 + me.y for i in range(4)]
    a_stat = push(stats.at[:, pl.ds((1 - me.c) * 2, 2)], sa, a_send.at[8], a_recv.at[8], partner)
    go(a_stat)
    a = [push(o.at[order[i], theirs, USED], ra.at[i, :, USED], a_send.at[i], a_recv.at[i], partner) for i in range(8)]
    for copy in a:
        go(copy)

    def weights_of(m_list, l_list):
        top = m_list[0]
        for m in m_list[1:]:
            top = jnp.maximum(top, m)
        scale = [jnp.exp(m - top) for m in m_list]
        total = scale[0] * l_list[0]
        for f, l in zip(scale[1:], l_list[1:]):
            total = total + f * l
        return top, total, scale

    def blend(stat_refs, out_ref=None, divide=False):
        factors = []
        for half in range(2):
            top, total, scale = weights_of([r(0, half) for r in stat_refs], [r(1, half) for r in stat_refs])
            if out_ref is not None:
                out_ref[0, half], out_ref[1, half] = top, total
            factors.append([f / total for f in scale] if divide else scale)
        return factors

    def merge(head, factors, sources, store):
        turned = [pltpu.roll(f, lax.rem(128 - head, 128), 1) for f in factors]
        for bb in range(16):
            total = None
            for f, source in zip(turned, sources):
                term = source(bb) * jnp.broadcast_to(f[:, bb * 8:bb * 8 + 1], (8, 128))
                total = term if total is None else total + term
            store(bb, total)

    def of(ref, i, h):
        return lambda bb: ref[i, h * 16 + bb]

    def into(ref, i, h):
        def store(bb, value):
            ref[i, h * 16 + bb] = value
        return store

    def unit(ref, i, h):
        return ref.at[i, h * 16:h * 16 + 16, USED]

    def stat(ref):
        return lambda s, half: ref[s, half]

    a_stat.wait_recv()
    by_core = blend([lambda s, half: stats[s, me.c * 2 + half], stat(sa)], sma)
    b_stat = push(sma, sb, s_send.at[0], s_recv.at[0], y_peer)
    go(b_stat)
    b = [[push(unit(ma, i, h), unit(rb, i, h), b_send.at[i, h], b_recv.at[i, h], y_peer) for h in range(2)]
         for i in range(4)]
    for i in range(8):
        a[i].wait_recv()
        for h in range(2):
            merge(order[i], by_core[h],
                  [lambda bb, h=h, i=i: o[order[i], me.c * 32 + h * 16 + bb], of(ra, i, h)], into(ma, i, h))
            if i < 4:
                go(b[i][h])

    b_stat.wait_recv()
    by_y = blend([stat(sma), stat(sb)], smb)
    m_stat = push(smb, sm, s_send.at[1], s_recv.at[1], mate)
    go(m_stat)
    m = [[push(unit(mb, i, h), unit(rm, i, h), m_send.at[i, h], m_recv.at[i, h], mate) for h in range(2)]
         for i in range(3)]
    f = [[push(unit(mc, i, h), rf.at[h * 16:h * 16 + 16, USED], f_send.at[i, h], f_recv.at[h], peer)
          for h in range(2)] for i, peer in enumerate((far_end, far_inner))]
    f_stat = [push(smc, sf, s_send.at[2 + i], s_recv.at[2], peer) for i, peer in enumerate((far_end, far_inner))]

    def y_step(i, h):
        b[i][h].wait_recv()
        merge(order[4 + i], by_y[h], [of(ma, 4 + i, h), of(rb, i, h)], into(mb, i, h))
        if i < 2:
            if_end(lambda: go(m[i][h], at_end))
        elif i == 2:
            go(m[i][h])

    by_half = []

    def m_start():
        m_stat.wait_recv()
        by_half.extend(blend([stat(smb), stat(sm)], smc))
        for copy in f_stat:
            go(copy, at_inner)

    def m_step(i, h):
        m[i][h].wait_recv()
        merge(order[4 + i], by_half[h], [of(mb, i, h), of(rm, i, h)], into(mc, i, h))
        go(f[i][h], at_inner)

    y_step(0, 0)
    y_step(0, 1)
    y_step(1, 0)
    y_step(1, 1)

    @if_inner
    def _():
        by_half.clear()
        m_start()
        m_step(0, 0)
        m_step(0, 1)
    y_step(2, 0)

    def again():
        by_half.clear()
        by_half.extend(blend([stat(smb), stat(sm)]))

    @if_inner
    def _():
        again()
        m_step(1, 0)
    y_step(2, 1)

    @if_inner
    def _():
        again()
        m_step(1, 1)
    y_step(3, 0)
    y_step(3, 1)

    if_end(m_stat.wait_recv)
    f_stat[0].wait_recv()
    by_z = blend([stat(smb), stat(sm), stat(sf)], divide=True)
    for h in range(2):
        m[2][h].wait_recv()
        f[0][h].wait_recv()

        def final(bb, value, h=h):
            fin[pl.ds(h * 128 + bb * 8, 8), :] = value

        merge(order[7], by_z[h], [of(mb, 3, h), of(rm, 2, h), lambda bb, h=h: rf[h * 16 + bb]], final)
    for t in range(7):
        lhs[mine, t * 128:(t + 1) * 128] = fin[pl.ds(t, 32, stride=8), :].astype(BF16)
    d_copy = push(lhs.at[mine], lhs.at[mine], d_send, d_recv, partner)
    go(d_copy)
    for copy in w_copies:
        copy.wait()
    push(lhs.at[theirs], lhs.at[theirs], d_send, d_recv, partner).wait_recv()

    def rows_of(j):
        return pl.ds(pl.multiple_of(j * 8, 8), 8)

    quarter = HALF // 2

    def cols_of(h):
        return pl.ds(h * quarter, quarter)

    b2 = [[push(p.at[rows_of(order[i]), cols_of(h)], rb2.at[i, h], b2_send.at[i, h], b2_recv.at[i, h], y_peer)
           for h in range(2)] for i in range(4)]
    m2 = [[push(mb2.at[i, h], rm2.at[i, h], m2_send.at[i, h], m2_recv.at[i, h], mate) for h in range(2)]
          for i in range(3)]
    f2 = [[push(mc2.at[i, h], rf2.at[h], f2_send.at[i, h], f2_recv.at[h], peer) for h in range(2)]
          for i, peer in enumerate((far_end, far_inner))]
    for h in range(2):
        for n in range(2):
            at = h * quarter + n * (quarter // 2)
            p[:, at:at + quarter // 2] = jnp.dot(lhs[...], wbuf[:, at:at + quarter // 2], preferred_element_type=F32)
        for i in range(4):
            go(b2[i][h])

    def y2_step(i, h):
        b2[i][h].wait_recv()
        mb2[i, h] = p[rows_of(order[4 + i]), h * quarter:(h + 1) * quarter] + rb2[i, h]
        if i < 2:
            if_end(lambda: go(m2[i][h], at_end))
        elif i == 2:
            go(m2[i][h])

    def m2_step(i, h):
        m2[i][h].wait_recv()
        mc2[i, h] = mb2[i, h] + rm2[i, h]
        go(f2[i][h], at_inner)

    def part(j, c, h):
        return out.at[rows_of(j), pl.ds(pl.multiple_of(c * HALF + h * quarter, 128), quarter)]

    whole = Gather(me, lambda j, h: part(j, me.c, h), lambda j, h: part(j, 1 - me.c, h), sems)
    for h in range(2):
        for i in range(4):
            y2_step(i, h)
            if i == 2:
                @if_inner
                def _():
                    m2_step(0, h)
        if_inner(lambda: m2_step(1, h))
    for h in range(2):
        m2[2][h].wait_recv()
        f2[0][h].wait_recv()
        total = (mb2[3, h] + rm2[2, h]) + rf2[h]
        out[rows_of(me.j), pl.ds(pl.multiple_of(me.c * HALF + h * quarter, 128), quarter)] = total.astype(BF16)
        whole.start(h)
    whole.finish()
    for copy in started:
        copy.wait_send()

    @if_end
    def _():
        for copy in at_end:
            copy.wait_send()

    @if_inner
    def _():
        for copy in at_inner:
            copy.wait_send()


def dma(*shape):
    return pltpu.SemaphoreType.DMA(shape) if shape else pltpu.SemaphoreType.DMA


def solution(mesh):
    cache_spec = P('rep', 'seq', None, None)
    in_specs = (P('rep', None), P(), P(), P(), P('seq', None), cache_spec, cache_spec, P('rep'))
    out_specs = (P('rep', None), cache_spec, cache_spec)
    shape = jax.ShapeDtypeStruct

    def step(x, wq, wk, wv, wo, k, v, pos):
        cache = (64, 512, 128)
        g, wox, k2, v2 = pl.pallas_call(
            project_kernel,
            out_shape=[pltpu.VMEM((8, 9, 64, 128), BF16), shape((ROWS, HALF), BF16), pltpu.VMEM(cache, BF16),
                       pltpu.VMEM(cache, BF16)],
            in_specs=[HBM] * 7,
            out_specs=[VMEM, HBM, VMEM, VMEM],
            scratch_shapes=[pltpu.VMEM((64, D), BF16), pltpu.VMEM((D, 640), BF16), dma(), dma(2, CHUNKS, 2), dma(2), dma(),
                            dma()] + GATHER_SEMS,
            cost_estimate=pl.CostEstimate(flops=10 ** 10, bytes_accessed=10 ** 7, transcendentals=0),
            compiler_params=pltpu.CompilerParams(
                collective_id=1, has_side_effects=True, vmem_limit_bytes=32 * 2 ** 20),
            name='project',
        )(*[pltpu.with_memory_space_constraint(a, pltpu.HBM)
            for a in (x, wq, wk, wv, wo, k.reshape(cache), v.reshape(cache))])
        _, _, ko, vo, o, stats = pl.pallas_call(
            attend_kernel,
            out_shape=[pltpu.VMEM(cache, BF16), pltpu.VMEM(cache, BF16), shape(cache, BF16), shape(cache, BF16),
                       shape((8, 64, 8, 128), F32), shape((2, 4, 8, 128), F32)],
            in_specs=[SMEM, VMEM, VMEM, VMEM],
            out_specs=[VMEM, VMEM, HBM, HBM, VMEM, VMEM],
            input_output_aliases={2: 0, 3: 1},
            scratch_shapes=[pltpu.VMEM((64 * PITCH, 128), F32), pltpu.VMEM((8 * PITCH, 128), F32), dma(4), dma(4)],
            cost_estimate=pl.CostEstimate(flops=2 * 10 ** 9, bytes_accessed=4 * 10 ** 7, transcendentals=0),
            compiler_params=pltpu.CompilerParams(vmem_limit_bytes=30 * 2 ** 20),
            name='attend',
        )(pos, g, k2, v2)
        piece = (32, 8, 128)
        stat = pltpu.VMEM((2, 2, 8, 128), F32)

        def pieces(n):
            return pltpu.VMEM((n,) + piece, F32)

        def sums(n):
            return pltpu.VMEM((n, 2, 8, HALF // 2), F32)

        y = pl.pallas_call(
            combine_kernel,
            out_shape=shape((64, D), BF16),
            in_specs=[VMEM, VMEM, HBM, HBM],
            out_specs=VMEM,
            scratch_shapes=[
                pieces(8), stat, pieces(8), stat, pieces(4), stat, pieces(4), stat, pieces(3), stat, pieces(2), stat,
                pltpu.VMEM(piece, F32), stat,
                pltpu.VMEM((256, 128), F32), pltpu.VMEM((64, 896), BF16), pltpu.VMEM((896, HALF), BF16),
                pltpu.VMEM((64, HALF), F32), sums(4), sums(4), sums(3), sums(2), pltpu.VMEM((2, 8, HALF // 2), F32),
                dma(2), dma(9), dma(9), dma(4, 2), dma(4, 2), dma(3, 2), dma(3, 2), dma(2, 2), dma(2),
                dma(4), dma(3), dma(), dma(), dma(4, 2), dma(4, 2), dma(3, 2), dma(3, 2), dma(2, 2), dma(2),
            ] + GATHER_SEMS,
            cost_estimate=pl.CostEstimate(flops=10 ** 10, bytes_accessed=10 ** 7, transcendentals=0),
            compiler_params=pltpu.CompilerParams(
                collective_id=2, has_side_effects=True, vmem_limit_bytes=28 * 2 ** 20),
            name='combine',
        )(o, stats, pltpu.with_memory_space_constraint(wo, pltpu.HBM), wox)
        return y, ko.reshape(k.shape), vo.reshape(v.shape)

    return jax.shard_map(step, mesh=mesh, in_specs=in_specs, out_specs=out_specs, check_vma=False)
```

time: 89.3 us -> 81 us (0.907)
  Pallas kernels: 86.4 us -> 79.3 us
  local copies, waits for them, and re-layouts: 2.1 us -> 0.93 us
    pallas_call x1, Pallas kernels: 55.5 us -> 47.4 us  [step(): pl.pallas_call(combine_kernel, out_shape=shape((64, D), BF16), in_specs=[...]
    unnamed x5 -> x3, local copies, waits for them, and re-layouts: 2.1 us -> 0.93 us
    pallas_call x1, Pallas kernels: 20.5 us -> 21.5 us  [step(): pl.pallas_call(project_kernel, out_shape=[pltpu.VMEM((8, 9, 64, 128), BF1...]
where the time goes in v3:
time: 81 us; the launch traced here: 80.9 us
  Pallas kernels  79.3 us (98%)
  local copies, waits for them, and re-layouts  0.93 us (1%)
    pallas_call x1, Pallas kernels, step(): pl.pallas_call(combine_kernel, out_shape=shape((64, D), BF16), in_specs=[...  47.4 us
    pallas_call x1, Pallas kernels, step(): pl.pallas_call(project_kernel, out_shape=[pltpu.VMEM((8, 9, 64, 128), BF1...  21.5 us
    pallas_call x1, Pallas kernels, step(): pl.pallas_call(attend_kernel, out_shape=[pltpu.VMEM(cache, BF16), pltpu.V...  10.4 us

profile of v3, /device:TPU:0, one launch (start us, length us, event | category | flops | bytes accessed | tf_op | source)
XLA Modules:
  0.0 80.9 jit_solution(13056141000852028425)
XLA Ops:
  0.6 0.0 copy-start
  0.6 21.5 %project.1 = (bf16[8,9,64,128]{3,2,1,0:T(8,128)(2,1)S(1)}, bf16[448,3584]{1,0:T(8,128)(2,1)S(1)}, bf16[64,512,128]{2,1,0:T(8,128)(2,1)S(1)}, bf16[64,512,128]{2,1,0:T(8,128)(2,1)S(1)}) custom-call(bf16[64,7168]{1,0:T(8,128)(2,1)} %x_in.1, bf16[7168,7168]{1,0:T(8,128)(2,1)} %wq.1, bf16[7168,1024]{1,0:T(8,128)(2,1)} %wk.1, bf16[7168,1024]{1,0:T(8,128)(2,1)} %wv.1, ...), custom_call_target="tpu_custom_call" | custom-call | flops 10000000000 | bytes 10000000 | tf_op jit(solution)/shard_map/project/pallas_call | solution.py:529
  22.1 0.0 copy-done
  22.2 10.4 %attend.1 = (bf16[64,512,128]{2,1,0:T(8,128)(2,1)S(1)}, bf16[64,512,128]{2,1,0:T(8,128)(2,1)S(1)}, bf16[64,512,128]{2,1,0:T(8,128)(2,1)}, bf16[64,512,128]{2,1,0...) custom-call(s32[64]{0:T(128)S(1)} %copy-done, ...), custom_call_target="tpu_custom_call", output_to_operand_aliasing={{0}: (2, {}), {1}: (3, {})} | custom-call | flops 2000000000 | bytes 40000000 | tf_op jit(solution)/shard_map/attend/pallas_call | solution.py:543
  32.6 47.4 %combine.1 = bf16[64,7168]{1,0:T(8,128)(2,1)S(1)} custom-call(f32[8,64,8,128]{3,2,1,0:T(8,128)S(1)} %get-tuple-element.14.o, f32[2,4,8,128]{3,2,1,0:T(8,128)S(1)} %get-tuple-element.15.stats, bf16[448,7168]{1,0:T(8,128)(2,1)} %wo.3, bf16[448,3584]{1,0:T(8,128)(2,1)S(1)} %get-tuple-element.16.wox), custom_call_target="tpu_custom_call" | custom-call | flops 10000000000 | bytes 10000000 | tf_op jit(solution)/shard_map/combine/pallas_call | solution.py:564
  79.9 0.9 %copy.16 = bf16[64,7168]{1,0:T(8,128)(2,1)} copy(bf16[64,7168]{1,0:T(8,128)(2,1)S(1)} %combine.1) | data formatting | bytes 1835008
Async XLA Ops:
  0.6 21.5 %copy-start = (s32[64]{0:T(128)S(1)}, s32[64]{0:T(128)}, u32[]{:S(2)}) copy-start(s32[64]{0:T(128)} %pos.1) | copy-start | bytes 772

commit v4 on v0

v4 whole, which is shorter than its diff:
```python
import functools

import jax
import jax.numpy as jnp
from jax import lax
from jax.experimental import pallas as pl
from jax.experimental.pallas import tpu as pltpu
from jax.sharding import PartitionSpec as P

MESH = pl.DeviceIdType.MESH
F32, BF16 = jnp.float32, jnp.bfloat16
VMEM = pl.BlockSpec(memory_space=pltpu.VMEM)
HBM = pl.BlockSpec(memory_space=pltpu.HBM)
SMEM = pl.BlockSpec(memory_space=pltpu.SMEM)
LOWEST = float(jnp.finfo(jnp.float32).min)
LANES = 128
D = 7168
HALF = D // 2
ROWS = 448
CHUNKS = 4
GROUP = 1
SLICES = 4
PARTS = 4
USED = slice(0, 7)
BATCH = 16
PITCH = 65
CHUNK = D // CHUNKS


Y_STEPS = ('y00y01y10y11y20y21y02y03m00m01y12m10', 'y13m11y22m02y23m03y30m12y31m13y32y33')
OUT_STEPS = ('y00y10y01y11y02m00y12m10y03m01y13m11y20m02', 'y21m12y22m03y23m13y30f00y31f01y32f02y33f03')


def read_steps(lines):
    return [('ymf'.index(line[n]), int(line[n + 1]), int(line[n + 2])) for line in lines
            for n in range(0, len(line), 3)]


class Place:
    def __init__(self):
        self.rep = lax.axis_index('rep')
        seq = lax.axis_index('seq')
        self.z = seq // 4
        self.y = lax.rem(seq // 2, 2)
        self.c = lax.rem(seq, 2)
        self.j = seq // 2

    def at(self, z, y, c):
        return (self.rep, (z * 2 + y) * 2 + c)

    def others(self):
        z = self.z
        low = 1 - z // 2
        return [low * 3, 1 + low, z + 1 - 2 * lax.rem(z, 2), z]

    def inner(self):
        return jnp.logical_and(self.z >= 1, self.z <= 2)

    def greet(self):
        barrier = pltpu.get_barrier_semaphore()
        peers = [self.at(self.z, self.y, 1 - self.c), self.at(self.z, 1 - self.y, self.c)]
        peers += [self.at(zz, self.y, self.c) for zz in self.others()[:3]]
        for peer in peers:
            pl.semaphore_signal(barrier, inc=1, device_id=peer, device_id_type=MESH)
        pl.semaphore_wait(barrier, len(peers))


def push(src, dst, send, recv, device):
    copy = pltpu.make_async_remote_copy(
        src_ref=src, dst_ref=dst, send_sem=send, recv_sem=recv, device_id=device, device_id_type=MESH)
    return copy


class Gather:
    def __init__(self, me, region, other, sems):
        self.me, self.region, self.other = me, region, other
        self.z_send, self.z_recv, self.y_send, self.y_recv, self.c_send, self.c_recv = sems
        self.zs = me.others()

    def go(self, copy):
        copy.start()

    def along_z(self, h, i, j, arrival=False):
        src = self.region(j, h)
        slot = i if arrival or i == 2 else lax.rem((self.me.z + 1) // 2, 2)
        return push(src, src, self.z_send.at[h, i], self.z_recv.at[h, slot],
                    self.me.at(self.zs[i], self.me.y, self.me.c))

    def across_y(self, h, i, j):
        src = self.region(j, h)
        return push(src, src, self.y_send.at[h, i], self.y_recv.at[h, i],
                    self.me.at(self.me.z, 1 - self.me.y, self.me.c))

    def to_core(self, h, i, src):
        return push(src, src, self.c_send.at[h, i], self.c_recv.at[h, i],
                    self.me.at(self.me.z, self.me.y, 1 - self.me.c))

    def start(self, h):
        for i in range(3):
            self.go(self.along_z(h, i, self.me.j))
        self.go(self.across_y(h, 3, self.me.j))
        self.go(self.to_core(h, 3, self.region(self.me.j, h)))

    def near(self, i):
        return self.zs[i] * 2 + self.me.y

    def far(self, i):
        return self.zs[i] * 2 + 1 - self.me.y

    def from_z(self, h):
        for i in (2, 1, 0):
            self.along_z(h, i, self.near(i), arrival=True).wait_recv()
            self.go(self.across_y(h, i, self.near(i)))
            self.go(self.to_core(h, i, self.region(self.near(i), h)))

    def from_y(self, h):
        for i in (3, 2, 1, 0):
            self.across_y(h, i, self.far(i)).wait_recv()
            self.go(self.to_core(h, 4 + i, self.region(self.far(i), h)))

    def from_core(self, h):
        for i in (3, 2, 1, 0):
            self.to_core(h, i, self.other(self.near(i), h)).wait_recv()
            self.to_core(h, 4 + i, self.other(self.far(i), h)).wait_recv()

    def sent(self, h):
        for i in range(3):
            self.along_z(h, i, self.me.j).wait_send()
        for i in range(4):
            self.across_y(h, i, self.near(i)).wait_send()
            self.to_core(h, i, self.region(self.near(i), h)).wait_send()
            self.to_core(h, 4 + i, self.region(self.far(i), h)).wait_send()


def gather_sems(parts):
    return [pltpu.SemaphoreType.DMA((parts, n)) for n in (3, 3, 4, 4, 8, 8)]


TILES = ((0, 5), (5, 4))


def step_kernel(pos_in, x_in, wq, wk, wv, wo, k_in, v_in, out, k, v, kn, vn,
                g, x, wbuf, qs, vs, o, stats, ra, sa, ma, sma, rb, sb, mb, smb, rm, sm, mc, smc, rf, sf, fin, lhs,
                wbuf2, p, rb2, mb2, rm2, mc2, rf2,
                pos, pos_sem, x_sem, w_sem, kv_sem, wo_sem, swap_send, swap_recv, a_send, a_recv, b_send, b_recv, m_send, m_recv,
                f_send, f_recv, as_send, as_recv, bs_send, bs_recv, ms_send, ms_recv, fs_send, fs_recv,
                d_send, d_recv, b2_send, b2_recv, m2_send, m2_recv, f2_send, f2_recv, *sems):
    me = Place()
    zs = me.others()
    partner = me.at(me.z, me.y, 1 - me.c)
    y_peer = me.at(me.z, 1 - me.y, me.c)
    far_end, far_inner, mate = [me.at(zs[i], me.y, me.c) for i in range(3)]
    mine = pl.ds(pl.multiple_of(me.c * 32, 32), 32)
    theirs = pl.ds(pl.multiple_of((1 - me.c) * 32, 32), 32)
    started, at_end, at_inner = [], [], []

    def go(copy, kept=started):
        copy.start()
        kept.append(copy)

    def if_inner(f):
        pl.when(me.inner())(f)

    def if_end(f):
        pl.when(jnp.logical_not(me.inner()))(f)

    x_copy = pltpu.make_async_copy(x_in, x, x_sem)
    pos_copy = pltpu.make_async_copy(pos_in, pos, pos_sem)
    pos_copy.start()
    cache = []
    for i in range(SLICES):
        bs = slice(i * 64 // SLICES, (i + 1) * 64 // SLICES)
        cache += [pltpu.make_async_copy(k_in.at[bs], k.at[bs], kv_sem.at[0, i]),
                  pltpu.make_async_copy(v_in.at[bs], v.at[bs], kv_sem.at[1, i])]

    def weights(c, i):
        rows = pl.ds(i * CHUNK, CHUNK)
        if c == 0:
            parts = [(wq, me.j * 896, 640)]
        else:
            parts = [(wq, me.j * 896 + 640, 256), (wk, me.j * LANES, LANES), (wv, me.j * LANES, LANES)]
        at, copies = 0, []
        for n, (w, col, width) in enumerate(parts):
            copies.append(pltpu.make_async_copy(w.at[rows, pl.ds(pl.multiple_of(col, LANES), width)],
                                                wbuf.at[rows, at:at + width], w_sem.at[i, n]))
            at += width
        return copies

    for c in range(2):
        @pl.when(me.c == c)
        def _(c=c):
            for i in range(CHUNKS):
                for copy in weights(c, i):
                    copy.start()
                if i == 0:
                    x_copy.start()

    me.greet()
    x_copy.wait()
    for c in range(2):
        @pl.when(me.c == c)
        def _(c=c):
            lo, n = TILES[c]
            acc = jnp.zeros((64, n * LANES), F32)
            rows = GROUP * CHUNK
            for i in range(CHUNKS // GROUP):
                for u in range(GROUP):
                    for copy in weights(c, i * GROUP + u):
                        copy.wait()
                acc += jnp.dot(x[:, i * rows:(i + 1) * rows], wbuf[i * rows:(i + 1) * rows, :n * LANES],
                               preferred_element_type=F32)
            for h in range(2):
                for q in range(2):
                    for t in range(n):
                        g[h, me.j, lo + t, q * 16:q * 16 + 16] = acc[
                            q * 32 + h * 16:q * 32 + h * 16 + 16, t * LANES:(t + 1) * LANES].astype(BF16)

    wo_copy = pltpu.make_async_copy(wo.at[:, pl.ds(pl.multiple_of(me.c * HALF, LANES), HALF)],
                                    wbuf2.at[pl.ds(pl.multiple_of(me.c * ROWS, 64), ROWS)], wo_sem)
    swap = push(wo.at[:, pl.ds(pl.multiple_of((1 - me.c) * HALF, LANES), HALF)],
                wbuf2.at[pl.ds(pl.multiple_of(me.c * ROWS, 64), ROWS)], swap_send, swap_recv, partner)

    def begin_caches():
        for copy in cache:
            copy.start()
        wo_copy.start()
        swap.start()

    def inputs(f):
        for c in range(2):
            @pl.when(me.c == c)
            def _(c=c):
                lo, n = TILES[c]
                lo2, n2 = TILES[1 - c]
                f(Gather(me, lambda j, h: g.at[h, j, lo:lo + n], lambda j, h: g.at[h, j, lo2:lo2 + n2], sems[:6]))

    def gather_first(w):
        w.start(0)
        w.start(1)

    def gather_relay(w):
        w.from_z(0)
        w.from_z(1)
        w.from_y(0)
        w.from_core(0)

    def gather_last(w):
        w.from_core(1)
        w.sent(0)
        w.sent(1)

    inputs(gather_first)
    begin_caches()
    inputs(gather_relay)
    for copy in cache:
        copy.wait()
    pos_copy.wait()

    first = lax.axis_index('seq') * 64
    s_of = lax.broadcasted_iota(jnp.int32, (8, LANES), 1) // 8
    lane = lax.broadcasted_iota(jnp.int32, (8, 512), 1)
    is_head = [lax.rem(lane, 8) == n for n in range(8)]
    at_of = lane // 8
    row_of = lax.broadcasted_iota(jnp.int32, (512, LANES), 0) // 8

    def spread(h):
        def head(j, _):
            for t in range(8):
                qs[pl.ds((j * 8 + t) * PITCH + h * 32, 32), :] = g[h, j, t].astype(F32)
            vs[pl.ds(j * PITCH + h * 32, 32), :] = g[h, j, 8].astype(F32)
            return 0

        lax.fori_loop(0, 8, head, 0)

        def news(e, _):
            at = h * 32 + e
            for to, new in ((kn, qs[pl.ds(7 * PITCH + at, 8, stride=8 * PITCH), :]),
                            (vn, vs[pl.ds(at, 8, stride=PITCH), :])):
                to[at] = jnp.concatenate([new, new], axis=0).astype(BF16)
            return 0

        lax.fori_loop(0, 32, news, 0, unroll=8)

    def with_new(ref, b, new, limit):
        return jnp.where(row_of == limit, jnp.concatenate([new] * 32, axis=0), ref[b])

    def scores(b, at):
        q = qs[pl.ds(at, 64, stride=PITCH), :].astype(BF16)
        limit = pos[b] - first
        s = lax.dot_general(q, with_new(k, b, kn[at], limit), (((1,), (1,)), ((), ())), preferred_element_type=F32)
        t = s[0:8]
        for hd in range(1, 8):
            t = jnp.where(is_head[hd], s[hd * 8:hd * 8 + 8], t)
        valid = at_of <= limit
        return jnp.where(valid, t * (LANES ** -0.5), LOWEST), valid

    def quarters(a):
        return [a[:, n * LANES:(n + 1) * LANES] for n in range(4)]

    def soften(batch):
        m = []
        for t, _ in batch:
            q = quarters(t)
            m.append(jnp.maximum(jnp.maximum(q[0], q[1]), jnp.maximum(q[2], q[3])))
        for shift in (8, 16, 32, 64):
            turned = [pltpu.roll(a, shift, 1) for a in m]
            m = [jnp.maximum(a, b) for a, b in zip(m, turned)]
        e = [jnp.where(valid, jnp.exp(t - jnp.concatenate([a] * 4, axis=1)), 0.0) for (t, valid), a in zip(batch, m)]
        l = []
        for w in e:
            q = quarters(w)
            l.append((q[0] + q[1]) + (q[2] + q[3]))
        for shift in (8, 16, 32, 64):
            turned = [pltpu.roll(a, shift, 1) for a in l]
            l = [a + b for a, b in zip(l, turned)]
        return m, l, e

    def values(b, at, e):
        w = jnp.concatenate([jnp.where(is_head[hd], e, 0.0) for hd in range(8)], axis=0).astype(BF16)
        ob = jnp.dot(w, with_new(v, b, vn[at], pos[b] - first), preferred_element_type=F32)
        for hd in range(8):
            o[hd, b] = ob[hd * 8:hd * 8 + 8]

    def attend(h, q):
        places = [(q * 32 + h * 16 + e, h * 32 + q * 16 + e) for e in range(16)]
        ahead = [scores(*place) for place in places[:BATCH]]
        ms = ls = jnp.zeros((8, LANES), F32)
        for i in range(16 // BATCH):
            batch, ahead = ahead, []
            if i + 1 < 16 // BATCH:
                ahead = [scores(*place) for place in places[(i + 1) * BATCH:(i + 2) * BATCH]]
            m, l, w = soften(batch)
            for e in range(BATCH):
                bb = i * BATCH + e
                values(*places[bb], w[e])
                here = s_of == bb
                ms, ls = jnp.where(here, m[e], ms), jnp.where(here, l[e], ls)
        stats[0, q * 2 + h] = ms
        stats[1, q * 2 + h] = ls

    order = [zs[i] * 2 + 1 - me.y for i in range(4)] + [zs[i] * 2 + me.y for i in range(4)]
    a_stat = [push(stats.at[:, (1 - me.c) * 2 + h], sa.at[:, h], as_send.at[h], as_recv.at[h], partner)
              for h in range(2)]
    a = [[push(o.at[order[i], pl.ds((1 - me.c) * 32 + h * 16, 16), USED], ra.at[i, h * 16:h * 16 + 16, USED],
               a_send.at[i, h], a_recv.at[i, h], partner) for h in range(2)] for i in range(8)]

    def exchange(h):
        go(a_stat[h])
        for i in range(8):
            go(a[i][h])

    def weights_of(m_list, l_list):
        top = m_list[0]
        for m in m_list[1:]:
            top = jnp.maximum(top, m)
        scale = [jnp.exp(m - top) for m in m_list]
        total = scale[0] * l_list[0]
        for f, l in zip(scale[1:], l_list[1:]):
            total = total + f * l
        return top, total, scale

    def blend(stat_refs, h, out_ref=None, divide=False):
        top, total, scale = weights_of([r(0, h) for r in stat_refs], [r(1, h) for r in stat_refs])
        if out_ref is not None:
            out_ref[0, h], out_ref[1, h] = top, total
        return [f / total for f in scale] if divide else scale

    def merge(head, q, factors, sources, store):
        turned = [pltpu.roll(f, lax.rem(LANES - head, LANES), 1) for f in factors]
        for bb in range(8):
            total = None
            lane0 = (q % 2 * 8 + bb) * 8
            for f, source in zip(turned, sources):
                term = source(q * 8 + bb) * jnp.broadcast_to(f[:, lane0:lane0 + 1], (8, LANES))
                total = term if total is None else total + term
            store(q * 8 + bb, total)

    def of(ref, i):
        return lambda b: ref[i, b]

    def into(ref, i):
        def store(b, value):
            ref[i, b] = value
        return store

    def unit(ref, i, q):
        return ref.at[i, q * 8:q * 8 + 8, USED]

    def stat(ref):
        return lambda s, h: ref[s, h]

    b_stat = [push(sma.at[:, h], sb.at[:, h], bs_send.at[h], bs_recv.at[h], y_peer) for h in range(2)]
    b = [[push(unit(ma, i, q), unit(rb, i, q), b_send.at[i, q], b_recv.at[i, q], y_peer) for q in range(PARTS)]
         for i in range(4)]
    by_core = [None, None]

    def core_step(h, some):
        if by_core[h] is None:
            a_stat[h].wait_recv()
            by_core[h] = blend([lambda s, h: stats[s, me.c * 2 + h], stat(sa)], h, sma)
            go(b_stat[h])
        for i in some:
            a[i][h].wait_recv()
        for i in some:
            for q in (2 * h, 2 * h + 1):
                merge(order[i], q, by_core[h], [lambda bb, i=i: o[order[i], me.c * 32 + bb], of(ra, i)], into(ma, i))
        for i in some:
            if i < 4:
                go(b[i][2 * h])
                go(b[i][2 * h + 1])

    spread(0)
    attend(0, 1 - me.c)
    inputs(lambda w: w.from_y(1))
    exchange(0)
    attend(0, me.c)
    core_step(0, range(3))
    inputs(gather_last)
    spread(1)
    attend(1, 1 - me.c)
    exchange(1)
    attend(1, me.c)
    core_step(1, range(3))
    core_step(0, range(3, 8))
    core_step(1, range(3, 8))

    m_stat = [push(smb.at[:, h], sm.at[:, h], ms_send.at[h], ms_recv.at[h], mate) for h in range(2)]
    m = [[push(unit(mb, i, q), unit(rm, i, q), m_send.at[i, q], m_recv.at[i, q], mate) for q in range(PARTS)]
         for i in range(3)]
    f = [[push(unit(mc, i, q), rf.at[q * 8:q * 8 + 8, USED], f_send.at[i, q], f_recv.at[q], peer)
          for q in range(PARTS)] for i, peer in enumerate((far_end, far_inner))]
    f_stat = [[push(smc.at[:, h], sf.at[:, h], fs_send.at[i, h], fs_recv.at[h], peer) for h in range(2)]
              for i, peer in enumerate((far_end, far_inner))]
    by_y = [None, None]

    def y_step(i, q):
        h = q // 2
        if by_y[h] is None:
            b_stat[h].wait_recv()
            by_y[h] = blend([stat(sma), stat(sb)], h, smb)
            go(m_stat[h])
        b[i][q].wait_recv()
        merge(order[4 + i], q, by_y[h], [of(ma, 4 + i), of(rb, i)], into(mb, i))
        if i < 2:
            if_end(lambda: go(m[i][q], at_end))
        elif i == 2:
            go(m[i][q])

    def m_step(i, q):
        h = q // 2
        opens = i == 0 and q % 2 == 0
        if opens:
            m_stat[h].wait_recv()
        factors = blend([stat(smb), stat(sm)], h, smc if opens else None)
        if opens:
            for copy in f_stat:
                go(copy[h], at_inner)
        m[i][q].wait_recv()
        merge(order[4 + i], q, factors, [of(mb, i), of(rm, i)], into(mc, i))
        go(f[i][q], at_inner)

    for inner, i, q in read_steps(Y_STEPS):
        if not inner:
            y_step(i, q)
        else:
            if_inner(lambda: m_step(i, q))

    for q in range(PARTS):
        h = q // 2
        if q % 2 == 0:
            if_end(m_stat[h].wait_recv)
            f_stat[0][h].wait_recv()
            by_z = blend([stat(smb), stat(sm), stat(sf)], h, divide=True)
        m[2][q].wait_recv()
        f[0][q].wait_recv()

        def final(b, value):
            fin[pl.ds(b * 8, 8), :] = value

        merge(order[7], q, by_z, [of(mb, 3), of(rm, 2), lambda b: rf[b]], final)
    for t in range(7):
        lhs[mine, t * LANES:(t + 1) * LANES] = fin[pl.ds(t, 32, stride=8), :].astype(BF16)
    d_copy = push(lhs.at[mine], lhs.at[mine], d_send, d_recv, partner)
    go(d_copy)
    wo_copy.wait()
    swap.wait_send()
    push(wo.at[:, pl.ds(0, HALF)], wbuf2.at[pl.ds(pl.multiple_of((1 - me.c) * ROWS, 64), ROWS)], swap_send, swap_recv,
         partner).wait_recv()
    push(lhs.at[theirs], lhs.at[theirs], d_send, d_recv, partner).wait_recv()

    def rows_of(j):
        return pl.ds(pl.multiple_of(j * 8, 8), 8)

    width = HALF // PARTS

    def cols_of(q):
        return pl.ds(q * width, width)

    b2 = [[push(p.at[rows_of(order[i]), cols_of(q)], rb2.at[i, q], b2_send.at[i, q], b2_recv.at[i, q], y_peer)
           for q in range(PARTS)] for i in range(4)]
    m2 = [[push(mb2.at[i, q], rm2.at[i, q], m2_send.at[i, q], m2_recv.at[i, q], mate) for q in range(PARTS)]
          for i in range(3)]
    f2 = [[push(mc2.at[i, q], rf2.at[q], f2_send.at[i, q], f2_recv.at[q], peer) for q in range(PARTS)]
          for i, peer in enumerate((far_end, far_inner))]
    for q in range(PARTS):
        at = q * width
        p[:, at:at + width] = jnp.dot(lhs[...], wbuf2[:, at:at + width], preferred_element_type=F32)
        for i in range(2):
            go(b2[i][q])
    for i in range(2, 4):
        for q in range(PARTS):
            go(b2[i][q])

    def y2_step(i, q):
        b2[i][q].wait_recv()
        mb2[i, q] = p[rows_of(order[4 + i]), q * width:(q + 1) * width] + rb2[i, q]
        if i < 2:
            if_end(lambda: go(m2[i][q], at_end))
        elif i == 2:
            go(m2[i][q])

    def m2_step(i, q):
        m2[i][q].wait_recv()
        mc2[i, q] = mb2[i, q] + rm2[i, q]
        go(f2[i][q], at_inner)

    def part(j, c, q):
        return out.at[rows_of(j), pl.ds(pl.multiple_of(c * HALF + q * width, LANES), width)]

    whole = Gather(me, lambda j, q: part(j, me.c, q), lambda j, q: part(j, 1 - me.c, q), sems[6:])

    def finish(q):
        m2[2][q].wait_recv()
        f2[0][q].wait_recv()
        total = (mb2[3, q] + rm2[2, q]) + rf2[q]
        out[rows_of(me.j), pl.ds(pl.multiple_of(me.c * HALF + q * width, LANES), width)] = total.astype(BF16)
        whole.start(q)

    for kind, i, q in read_steps(OUT_STEPS):
        if kind == 0:
            y2_step(i, q)
        elif kind == 1:
            if_inner(lambda: m2_step(i, q))
        else:
            finish(q)
    for q in range(PARTS):
        whole.from_z(q)
    for q in range(PARTS):
        whole.from_y(q)
    for q in range(PARTS):
        whole.from_core(q)
    for q in range(PARTS):
        whole.sent(q)
    for copy in started:
        copy.wait_send()

    @if_end
    def _():
        for copy in at_end:
            copy.wait_send()

    @if_inner
    def _():
        for copy in at_inner:
            copy.wait_send()


def write_kernel(pos, kn, vn, k_in, v_in, k, v, ko, vo, k_sem, v_sem):
    first = lax.axis_index('seq') * 64

    def out(i):
        bs = pl.ds(i * 16, 16)
        return [pltpu.make_async_copy(k.at[bs], ko.at[bs], k_sem.at[i]),
                pltpu.make_async_copy(v.at[bs], vo.at[bs], v_sem.at[i])]

    for i in range(4):
        for e in range(16):
            b = i * 16 + e
            at = lax.rem(i, 2) * 32 + i // 2 * 16 + e
            row = pos[b] - first
            here = jnp.logical_and(row >= 0, row < 64)
            rows = pl.ds(pl.multiple_of(jnp.clip(row, 0, 63) * 8, 8), 8)
            k[b, rows, :] = jnp.where(here, kn[at, 0:8], k[b, rows, :])
            v[b, rows, :] = jnp.where(here, vn[at, 0:8], v[b, rows, :])
        for copy in out(i):
            copy.start()
    for i in range(4):
        for copy in out(i):
            copy.wait()


def dma(*shape):
    return pltpu.SemaphoreType.DMA(shape) if shape else pltpu.SemaphoreType.DMA


def solution(mesh):
    cache_spec = P('rep', 'seq', None, None)
    in_specs = (P('rep', None), P(), P(), P(), P('seq', None), cache_spec, cache_spec, P('rep'))
    out_specs = (P('rep', None), cache_spec, cache_spec)
    shape = jax.ShapeDtypeStruct

    def step(x, wq, wk, wv, wo, k, v, pos):
        cache = (64, 512, LANES)
        rows = pltpu.VMEM((64, 16, LANES), BF16)
        piece = (32, 8, LANES)
        stat = pltpu.VMEM((2, 2, 8, LANES), F32)

        def pieces(n):
            return pltpu.VMEM((n,) + piece, F32)

        def sums(n):
            return pltpu.VMEM((n, PARTS, 8, HALF // PARTS), F32)

        held = [pltpu.with_memory_space_constraint(a, pltpu.HBM)
                for a in (pos, x, wq, wk, wv, wo, k.reshape(cache), v.reshape(cache))]
        y, k2, v2, kn, vn = pl.pallas_call(
            step_kernel,
            out_shape=[pltpu.VMEM((64, D), BF16), pltpu.VMEM(cache, BF16), pltpu.VMEM(cache, BF16), rows, rows],
            in_specs=[HBM] * 8,
            out_specs=[VMEM] * 5,
            scratch_shapes=[
                pltpu.VMEM((2, 8, 9, 32, LANES), BF16), pltpu.VMEM((64, D), BF16), pltpu.VMEM((D, 640), BF16),
                pltpu.VMEM((64 * PITCH, LANES), F32), pltpu.VMEM((8 * PITCH, LANES), F32),
                pltpu.VMEM((8, 64, 8, LANES), F32), pltpu.VMEM((2, 4, 8, LANES), F32),
                pieces(8), stat, pieces(8), stat, pieces(4), stat, pieces(4), stat, pieces(3), stat, pieces(2), stat,
                pltpu.VMEM(piece, F32), stat,
                pltpu.VMEM((256, LANES), F32), pltpu.VMEM((64, 896), BF16), pltpu.VMEM((896, HALF), BF16),
                pltpu.VMEM((64, HALF), F32), sums(4), sums(4), sums(3), sums(2), pltpu.VMEM((PARTS, 8, HALF // PARTS), F32),
                pltpu.SMEM((64,), jnp.int32), dma(), dma(), dma(CHUNKS, 3), dma(2, SLICES), dma(), dma(), dma(),
                dma(8, 2), dma(8, 2), dma(4, PARTS), dma(4, PARTS), dma(3, PARTS), dma(3, PARTS), dma(2, PARTS), dma(PARTS),
                dma(2), dma(2), dma(2), dma(2), dma(2), dma(2), dma(2, 2), dma(2),
                dma(), dma(), dma(4, PARTS), dma(4, PARTS), dma(3, PARTS), dma(3, PARTS), dma(2, PARTS), dma(PARTS),
            ] + gather_sems(2) + gather_sems(PARTS),
            cost_estimate=pl.CostEstimate(flops=10 ** 10, bytes_accessed=10 ** 7, transcendentals=0),
            compiler_params=pltpu.CompilerParams(
                collective_id=1, has_side_effects=True, vmem_limit_bytes=36 * 2 ** 20),
            name='attend_step',
        )(*held)
        _, _, ko, vo = pl.pallas_call(
            write_kernel,
            out_shape=[pltpu.VMEM(cache, BF16), pltpu.VMEM(cache, BF16), shape(cache, BF16), shape(cache, BF16)],
            in_specs=[SMEM, VMEM, VMEM, VMEM, VMEM],
            out_specs=[VMEM, VMEM, HBM, HBM],
            input_output_aliases={3: 0, 4: 1},
            scratch_shapes=[dma(4), dma(4)],
            cost_estimate=pl.CostEstimate(flops=10 ** 9, bytes_accessed=4 * 10 ** 7, transcendentals=0),
            compiler_params=pltpu.CompilerParams(vmem_limit_bytes=30 * 2 ** 20),
            name='write_caches',
        )(pos, kn, vn, k2, v2)
        return y, ko.reshape(k.shape), vo.reshape(v.shape)

    return jax.shard_map(step, mesh=mesh, in_specs=in_specs, out_specs=out_specs, check_vma=False)
```

time: 327 us -> 76.2 us (0.23)
  blocking collectives: 198 us -> 0 us
  Pallas kernels: 0 us -> 74.3 us
  matrix products: 60.6 us -> 0 us
  waiting for transfers between devices: 34.4 us -> 0 us
  between operations: 14.2 us -> 0.81 us
  other arithmetic: 13 us -> 0 us
  local copies, waits for them, and re-layouts: 6.63 us -> 0.93 us
    psum x2 -> x0, blocking collectives: 132 us -> none  [the longest x1 71.1 us: local_step(): result = lax.psum(part_out, 'seq').astype(jnp.bfloat16)]
    pallas_call x0 -> x2, Pallas kernels: none -> 74.3 us  [the longest x1 67.8 us: step(): pl.pallas_call(step_kernel, out_shape=[pltpu.VMEM((64, D), BF16), pltpu.V...]
    pmax x1 -> x0, blocking collectives: 65.3 us -> none  [local_step(): global_max = lax.pmax(local_max, 'seq')]
    dot_general x6 -> x0, matrix products: 60.6 us -> none  [the longest x1 35.3 us: local_step(): jnp.dot(hidden, w_query, preferred_element_type=jnp.float32)]
    psum x1 -> x0, waiting for transfers between devices: 34.3 us -> none  [local_step(): lax.psum((local_sum * rescale, local_out * rescale[..., None]), 'seq')]
    select_n x2 -> x0, other arithmetic: 9.58 us -> none  [the longest x1 9.55 us: local_step(): k_updated = jnp.where(at_pos, key_new[:, None], k_cache)]
    reshape x2 -> x0, local copies, waits for them, and re-layouts: 4.11 us -> none  [the longest x1 2.21 us: local_step(): q_heads = q_flat.reshape(batch_size, kv_heads, group_size, head_dim)]
  transfers between devices with their start and end apart: 1 -> 0, of which waited for: 1 -> 0; matrix products, arithmetic and copies ran while one was open for 0% -> 0% of each run, Pallas kernels for 0% -> 0%
where the time goes in v4:
time: 76.2 us; the launch traced here: 76.1 us
  Pallas kernels  74.3 us (98%)
  local copies, waits for them, and re-layouts  0.93 us (1%)
  between operations  0.81 us (1%)
    pallas_call x1, Pallas kernels, step(): pl.pallas_call(step_kernel, out_shape=[pltpu.VMEM((64, D), BF16), pltpu.V...  67.8 us
    pallas_call x1, Pallas kernels, step(): pl.pallas_call(write_kernel, out_shape=[pltpu.VMEM(cache, BF16), pltpu.VM...  6.55 us

profile of v4, /device:TPU:0, one launch (start us, length us, event | category | flops | bytes accessed | tf_op | source)
XLA Modules:
  0.0 76.1 jit_solution(6809795892248504613)
XLA Ops:
  0.6 0.0 copy-start
  0.6 67.8 %attend_step.1 = (bf16[64,7168]{1,0:T(8,128)(2,1)S(1)}, bf16[64,512,128]{2,1,0:T(8,128)(2,1)S(1)}, bf16[64,512,128]{2,1,0:T(8,128)(2,1)S(1)}, bf16[64,16,128]{2,1,0:T(8,128)(2,1)S(1)}, bf16[64,16,128]{2,1,0:T(8,128)(2,1)S(1)}) custom-call(s32[64]{0:T(128)} %pos.1, bf16[64,7168]{1,0:T(8,128)(2,1)} %x_in.1, bf16[7168,7168]{1,0:T(8,128)(2,1)} %wq.1, ...), custom_call_target="tpu_custom_call" | custom-call | flops 10000000000 | bytes 10000000 | tf_op jit(solution)/shard_map/attend_step/pallas_call | solution.py:616
  68.4 0.9 %copy.16 = bf16[64,7168]{1,0:T(8,128)(2,1)} copy(bf16[64,7168]{1,0:T(8,128)(2,1)S(1)} %get-tuple-element.17) | data formatting | bytes 1835008
  69.4 0.0 copy-done
  69.4 6.5 %write_caches.1 = (bf16[64,512,128]{2,1,0:T(8,128)(2,1)S(1)}, bf16[64,512,128]{2,1,0:T(8,128)(2,1)S(1)}, bf16[64,512,128]{2,1,0:T(8,128)(2,1)}, bf16[64,512,128]{2,1,0:T(8,128)(2,1)}) custom-call(s32[64]{0:T(128)S(1)} %copy-done, bf16[64,16,128]{2,1,0:T(8,128)(2,1)S(1)} %get-tuple-element.11.kn, ...), custom_call_target="tpu_custom_call", output_to_operand_aliasing={{0}: (3, {}), {1}: (4, {})} | custom-call | flops 1000000000 | bytes 40000000 | tf_op jit(solution)/shard_map/write_caches/pallas_call | solution.py:639
Async XLA Ops:
  0.6 68.7 %copy-start = (s32[64]{0:T(128)S(1)}, s32[64]{0:T(128)}, u32[]{:S(2)}) copy-start(s32[64]{0:T(128)} %pos.1) | copy-start | bytes 772

commit v5 on v4

--- a/solution.py
+++ b/solution.py
@@ -565,7 +565,9 @@
             copy.wait_send()
 
 
-def write_kernel(pos, kn, vn, k_in, v_in, k, v, ko, vo, k_sem, v_sem):
+def write_kernel(pos, kn, vn, y_in, k_in, v_in, k, v, ko, vo, y, k_sem, v_sem, y_sem):
+    y_copy = pltpu.make_async_copy(y_in, y, y_sem)
+    y_copy.start()
     first = lax.axis_index('seq') * 64
 
     def out(i):
@@ -587,6 +589,7 @@
     for i in range(4):
         for copy in out(i):
             copy.wait()
+    y_copy.wait()
 
 
 def dma(*shape):
@@ -636,17 +639,18 @@
                 collective_id=1, has_side_effects=True, vmem_limit_bytes=36 * 2 ** 20),
             name='attend_step',
         )(*held)
-        _, _, ko, vo = pl.pallas_call(
+        _, _, ko, vo, y = pl.pallas_call(
             write_kernel,
-            out_shape=[pltpu.VMEM(cache, BF16), pltpu.VMEM(cache, BF16), shape(cache, BF16), shape(cache, BF16)],
-            in_specs=[SMEM, VMEM, VMEM, VMEM, VMEM],
-            out_specs=[VMEM, VMEM, HBM, HBM],
-            input_output_aliases={3: 0, 4: 1},
-            scratch_shapes=[dma(4), dma(4)],
+            out_shape=[pltpu.VMEM(cache, BF16), pltpu.VMEM(cache, BF16), shape(cache, BF16), shape(cache, BF16),
+                       shape((64, D), BF16)],
+            in_specs=[SMEM] + [VMEM] * 5,
+            out_specs=[VMEM, VMEM, HBM, HBM, HBM],
+            input_output_aliases={4: 0, 5: 1},
+            scratch_shapes=[dma(4), dma(4), dma()],
             cost_estimate=pl.CostEstimate(flops=10 ** 9, bytes_accessed=4 * 10 ** 7, transcendentals=0),
             compiler_params=pltpu.CompilerParams(vmem_limit_bytes=30 * 2 ** 20),
             name='write_caches',
-        )(pos, kn, vn, k2, v2)
+        )(pos, kn, vn, y, k2, v2)
         return y, ko.reshape(k.shape), vo.reshape(v.shape)
 
     return jax.shard_map(step, mesh=mesh, in_specs=in_specs, out_specs=out_specs, check_vma=False)

time: 76.2 us -> 75.6 us (level)
  local copies, waits for them, and re-layouts: 0.93 us -> 0.01 us
    unnamed x3 -> x2, local copies, waits for them, and re-layouts: 0.93 us -> 0.01 us
where the time goes in v5:
time: 75.6 us; the launch traced here: 75.4 us
  Pallas kernels  74.6 us (99%)
  between operations  0.82 us (1%)
    pallas_call x1, Pallas kernels, step(): pl.pallas_call(step_kernel, out_shape=[pltpu.VMEM((64, D), BF16), pltpu.V...  67.8 us
    pallas_call x1, Pallas kernels, step(): pl.pallas_call(write_kernel, out_shape=[pltpu.VMEM(cache, BF16), pltpu.VM...  6.84 us

profile of v5, /device:TPU:0, one launch (start us, length us, event | category | flops | bytes accessed | tf_op | source)
XLA Modules:
  0.0 75.4 jit_solution(18042011089010289869)
XLA Ops:
  0.6 0.0 copy-start
  0.6 67.8 %attend_step.1 = (bf16[64,7168]{1,0:T(8,128)(2,1)S(1)}, bf16[64,512,128]{2,1,0:T(8,128)(2,1)S(1)}, bf16[64,512,128]{2,1,0:T(8,128)(2,1)S(1)}, bf16[64,16,128]{2,1,0:T(8,128)(2,1)S(1)}, bf16[64,16,128]{2,1,0:T(8,128)(2,1)S(1)}) custom-call(s32[64]{0:T(128)} %pos.1, bf16[64,7168]{1,0:T(8,128)(2,1)} %x_in.1, bf16[7168,7168]{1,0:T(8,128)(2,1)} %wq.1, ...), custom_call_target="tpu_custom_call" | custom-call | flops 10000000000 | bytes 10000000 | tf_op jit(solution)/shard_map/attend_step/pallas_call | solution.py:619
  68.4 0.0 copy-done
  68.4 6.8 %write_caches.1 = (bf16[64,512,128]{2,1,0:T(8,128)(2,1)S(1)}, bf16[64,512,128]{2,1,0:T(8,128)(2,1)S(1)}, bf16[64,512,128]{2,1,0:T(8,128)(2,1)}, bf16[64,512,128]{2,1,0:T(8,128)(2,1)}, bf16[64,7168]{1,0:T(8,128)(2,1)}) custom-call(s32[64]{0:T(128)S(1)} %copy-done, ...), custom_call_target="tpu_custom_call", output_to_operand_aliasing={{0}: (4, {}), {1}: (5, {})} | custom-call | flops 1000000000 | bytes 40000000 | tf_op jit(solution)/shard_map/write_caches/pallas_call | solution.py:642
Async XLA Ops:
  0.6 67.8 %copy-start = (s32[64]{0:T(128)S(1)}, s32[64]{0:T(128)}, u32[]{:S(2)}) copy-start(s32[64]{0:T(128)} %pos.1) | copy-start | bytes 772

commit v6 on v5

--- a/solution.py
+++ b/solution.py
@@ -27,7 +27,7 @@
 CHUNK = D // CHUNKS
 
 
-Y_STEPS = ('y00y01y10y11y20y21y02y03m00m01y12m10', 'y13m11y22m02y23m03y30m12y31m13y32y33')
+Y_STEPS = ('y00y01y10y11y20y21', 'y02y03m00m01y12m10y13m11y22m02y23m03y30m12y31m13y32y33')
 OUT_STEPS = ('y00y10y01y11y02m00y12m10y03m01y13m11y20m02', 'y21m12y22m03y23m13y30f00y31f01y32f02y33f03')
 
 
@@ -421,8 +421,7 @@
     exchange(1)
     attend(1, me.c)
     core_step(1, range(3))
-    core_step(0, range(3, 8))
-    core_step(1, range(3, 8))
+    core_step(0, range(4, 7))
 
     m_stat = [push(smb.at[:, h], sm.at[:, h], ms_send.at[h], ms_recv.at[h], mate) for h in range(2)]
     m = [[push(unit(mb, i, q), unit(rm, i, q), m_send.at[i, q], m_recv.at[i, q], mate) for q in range(PARTS)]
@@ -459,11 +458,15 @@
         merge(order[4 + i], q, factors, [of(mb, i), of(rm, i)], into(mc, i))
         go(f[i][q], at_inner)
 
-    for inner, i, q in read_steps(Y_STEPS):
-        if not inner:
-            y_step(i, q)
-        else:
-            if_inner(lambda: m_step(i, q))
+    for line in Y_STEPS:
+        for inner, i, q in read_steps((line,)):
+            if not inner:
+                y_step(i, q)
+            else:
+                if_inner(lambda: m_step(i, q))
+        if line is Y_STEPS[0]:
+            core_step(1, range(3, 8))
+            core_step(0, (3, 7))
 
     for q in range(PARTS):
         h = q // 2

time: 75.6 us -> 74.9 us (level)
  no operation moved by 1% of the time
where the time goes in v6:
time: 74.9 us; the launch traced here: 74.8 us
  Pallas kernels  74 us (99%)
  between operations  0.82 us (1%)
    pallas_call x1, Pallas kernels, step(): pl.pallas_call(step_kernel, out_shape=[pltpu.VMEM((64, D), BF16), pltpu.V...  67.1 us
    pallas_call x1, Pallas kernels, step(): pl.pallas_call(write_kernel, out_shape=[pltpu.VMEM(cache, BF16), pltpu.VM...  6.84 us

profile of v6, /device:TPU:0, one launch (start us, length us, event | category | flops | bytes accessed | tf_op | source)
XLA Modules:
  0.0 74.8 jit_solution(3439733912900800246)
XLA Ops:
  0.6 0.0 copy-start
  0.6 67.1 %attend_step.1 = (bf16[64,7168]{1,0:T(8,128)(2,1)S(1)}, bf16[64,512,128]{2,1,0:T(8,128)(2,1)S(1)}, bf16[64,512,128]{2,1,0:T(8,128)(2,1)S(1)}, bf16[64,16,128]{2,1,0:T(8,128)(2,1)S(1)}, bf16[64,16,128]{2,1,0:T(8,128)(2,1)S(1)}) custom-call(s32[64]{0:T(128)} %pos.1, bf16[64,7168]{1,0:T(8,128)(2,1)} %x_in.1, bf16[7168,7168]{1,0:T(8,128)(2,1)} %wq.1, ...), custom_call_target="tpu_custom_call" | custom-call | flops 10000000000 | bytes 10000000 | tf_op jit(solution)/shard_map/attend_step/pallas_call | solution.py:622
  67.8 0.0 copy-done
  67.8 6.8 %write_caches.1 = (bf16[64,512,128]{2,1,0:T(8,128)(2,1)S(1)}, bf16[64,512,128]{2,1,0:T(8,128)(2,1)S(1)}, bf16[64,512,128]{2,1,0:T(8,128)(2,1)}, bf16[64,512,128]{2,1,0:T(8,128)(2,1)}, bf16[64,7168]{1,0:T(8,128)(2,1)}) custom-call(s32[64]{0:T(128)S(1)} %copy-done, ...), custom_call_target="tpu_custom_call", output_to_operand_aliasing={{0}: (4, {}), {1}: (5, {})} | custom-call | flops 1000000000 | bytes 40000000 | tf_op jit(solution)/shard_map/write_caches/pallas_call | solution.py:645
Async XLA Ops:
  0.6 67.1 %copy-start = (s32[64]{0:T(128)S(1)}, s32[64]{0:T(128)}, u32[]{:S(2)}) copy-start(s32[64]{0:T(128)} %pos.1) | copy-start | bytes 772
